TPU v7x, 256 devices: a whole 4x4x8 slice. The times are simulated.
256 devices in a mesh: row: 4 (over x), col: 32 (over y, z), batch: 2 (over core).
Axes of the slice: x: 4, y: 4, z: 8, core: 2. Of those that a mesh axis runs over, the one named last changes fastest.
Arguments:
- item_ids: int32 [4, 32, 2048], P('batch', 'col', 'row'), parts along dimension 0, may hold values from 0 to 511
- pad_masks: int32 [4, 32, 2048], P('batch', 'col', 'row'), parts along dimension 0, may hold values from 0 to 1
- lengths: int32 [4], P('batch'), parts along dimension 0, may hold values from 64512 to 65536
- item_table: bfloat16 [512, 1024], replicated, may hold values from -5 to 5
- w_gate: bfloat16 [1024, 1024], replicated, may hold values from -0.1875 to 0.1875
- w_in: bfloat16 [1024, 1280], replicated, may hold values from -0.1875 to 0.1875
- w_dt: bfloat16 [1024, 8], replicated, may hold values from -0.1875 to 0.1875
- conv_taps: float32 [4, 1280], replicated, may hold values from -3 to 3
- dt_bias: float32 [8], replicated, may hold values from -2 to 1
- decay_rates: float32 [8], replicated, may hold values from 1.5258789e-06 to 0.05
- norm_gain: float32 [1024], replicated, may hold values from 0.1 to 1.9
- w_out: bfloat16 [1024, 1024], replicated, may hold values from -0.1875 to 0.1875
Outputs:
- result: bfloat16 [4, 32, 2048, 1024], P('batch', 'col', 'row'), parts along dimension 0
There are 2 independent parts, one for each index of `batch`. A program takes and returns all parts, laid end to end along the dimension named above; an argument that names none is the same for every part. Nothing has to cross between parts.
Inputs may be any that keep to these rules, and one draw needn't show every extreme that they name: `lengths`: every history keeps at least its first 64512 positions before padding.
All inputs are finite; a program needn't handle non-finite values.
Results may differ from a plain program's by a relative error of at most 0.0093.
Values may be sent and summed in bfloat16 or wider, within the bound.
A program may use at most 128 MiB of HBM per device.

v0:
```python
import jax
import jax.numpy as jnp
from jax import lax
from jax.sharding import Mesh
from jax.sharding import PartitionSpec as P

STRETCH = 128
COL = ("col_0", "col_1")


def passed_along(block, axis, distance):
    devices = range(lax.axis_size(axis))
    route = [((i - distance) % len(devices), i) for i in devices]
    return lax.ppermute(block, axis, route)


def from_behind(shard, axis, by):
    length = lax.axis_size(axis)
    pairs = [(i, i + by) for i in range(length) if 0 <= i + by < length]
    return lax.ppermute(shard, axis, pairs)


def nothing_yet(shard, identity):
    return jax.tree.map(
        lambda part, zero: jnp.zeros_like(part) + jnp.asarray(zero, part.dtype), shard, identity
    )


def carried_in(shard, axes, combine, identity):
    before = start = nothing_yet(shard, identity)
    subtotal = shard
    for axis in reversed(axes):
        length, index = (lax.axis_size(axis), lax.axis_index(axis))
        pieces = jax.tree.map(lambda part: lax.all_gather(part, axis), subtotal)
        inside, subtotal = (start, start)
        for k in range(length):
            passed = k < index
            subtotal = combine(subtotal, jax.tree.map(lambda part: part[k], pieces))
            inside = jax.tree.map(lambda new, old: jnp.where(passed, new, old), subtotal, inside)
        before = combine(inside, before)
    return before


def copy_for_each(shard, axis):
    copies = jnp.broadcast_to(shard, (lax.axis_size(axis), *shard.shape))
    return lax.all_to_all(copies, axis, split_axis=0, concat_axis=0, tiled=True)


def in_order(blocks, dim):
    shape = list(blocks.shape[1:])
    shape[dim] *= blocks.shape[0]
    return jnp.moveaxis(blocks, 0, dim).reshape(shape)


def gathered_copies(shard, axis, dim):
    blocks = copy_for_each(shard, axis)
    return in_order(blocks, dim)


def combine(earlier, later):
    return (earlier[0] + later[0], jnp.exp(-later[0])[..., None, None] * earlier[1] + later[1])


def choose_pair(condition, first_pair, second_pair):
    return (
        jnp.where(condition, first_pair[0], second_pair[0]),
        jnp.where(condition, first_pair[1], second_pair[1]),
    )


def per_device(
    item_ids,
    pad_masks,
    lengths,
    item_table,
    w_gate,
    w_in,
    w_dt,
    conv_taps,
    dt_bias,
    decay_rates,
    norm_gain,
    w_out,
):
    users = item_ids.shape[0]
    events = item_ids.shape[2]
    full_width = w_in.shape[1]
    inner_width = w_gate.shape[1]
    head_count = decay_rates.shape[0]
    head_size = inner_width // head_count
    state_width = (full_width - inner_width) // 2
    kernel = conv_taps.shape[0]
    row_count = lax.axis_size("row")
    row_place = lax.axis_index("row")
    col_place = lax.axis_index(COL)
    stretch_count = events // STRETCH
    item_rows = item_ids[:, 0, :]
    embedded = jnp.take(item_table, item_rows, axis=0).reshape(users * events, -1)
    projected = (
        jnp.dot(embedded, w_in, preferred_element_type=jnp.float32)
        .astype(jnp.bfloat16)
        .reshape(users, events, full_width)
    )
    gate_rows = (
        jnp.dot(embedded, w_gate, preferred_element_type=jnp.float32)
        .astype(jnp.bfloat16)
        .reshape(users, events, inner_width)
    )
    step_raw = jnp.dot(embedded, w_dt, preferred_element_type=jnp.float32).reshape(
        users, events, head_count
    )
    at_start = jnp.logical_and(row_place == 0, col_place == 0)
    tail_rows = projected[:, events - (kernel - 1) :, :]
    from_row = passed_along(tail_rows, "row", 1)
    from_col = from_behind(from_row, COL, 1)
    before = jnp.where(row_place == 0, from_col, from_row)
    before = jnp.where(at_start, jnp.zeros_like(before), before)
    joined = jnp.concatenate([before, projected], axis=1)
    convolved = joined[:, 0:events, :].astype(jnp.float32) * conv_taps[0]
    for offset in range(1, kernel):
        convolved = (
            convolved
            + joined[:, offset : offset + events, :].astype(jnp.float32) * conv_taps[offset]
        )
    signal = jax.nn.silu(convolved[..., :inner_width]).astype(jnp.bfloat16)
    inward = convolved[..., inner_width : inner_width + state_width].astype(jnp.bfloat16)
    outward = convolved[..., inner_width + state_width :].astype(jnp.bfloat16)
    first_event = (col_place * row_count + row_place) * events
    position = first_event + lax.broadcasted_iota(jnp.int32, (users, events), 1)
    usable = jnp.logical_and(position < lengths[:, None], pad_masks[:, 0, :] > 0).astype(
        jnp.float32
    )
    step_size = usable[..., None] * jax.nn.softplus(step_raw + dt_bias)
    log_decay = jnp.cumsum(
        (step_size * decay_rates).reshape(users, stretch_count, STRETCH, head_count), axis=2
    )
    log_heads = jnp.moveaxis(log_decay, 3, 2)
    size_heads = jnp.moveaxis(step_size.reshape(users, stretch_count, STRETCH, head_count), 3, 2)
    signal_heads = signal.reshape(users, stretch_count, STRETCH, head_count, head_size)
    inward_stretches = inward.reshape(users, stretch_count, STRETCH, state_width)
    outward_stretches = outward.reshape(users, stretch_count, STRETCH, state_width)
    scores = jnp.einsum(
        "scqn,scun->scqu", outward_stretches, inward_stretches, preferred_element_type=jnp.float32
    )
    causal = lax.broadcasted_iota(jnp.int32, (STRETCH, STRETCH), 0) >= lax.broadcasted_iota(
        jnp.int32, (STRETCH, STRETCH), 1
    )
    log_gap = log_heads[..., :, None] - log_heads[..., None, :]
    decays = jnp.where(causal, jnp.exp(-jnp.where(causal, log_gap, 0.0)), 0.0)
    weights = (scores[:, :, None] * decays * size_heads[:, :, :, None, :]).astype(jnp.bfloat16)
    local_out = jnp.einsum(
        "schqu,scuhp->scqhp", weights, signal_heads, preferred_element_type=jnp.float32
    )
    tail_weight = jnp.exp(log_heads - log_heads[..., -1:]) * size_heads
    scaled_in = (inward_stretches[:, :, None] * tail_weight[..., None]).astype(jnp.bfloat16)
    stretch_states = jnp.einsum(
        "schun,scuhp->schpn", scaled_in, signal_heads, preferred_element_type=jnp.float32
    )
    stretch_logs = log_heads[..., -1]
    running = (
        jnp.zeros((users, head_count), jnp.float32),
        jnp.zeros((users, head_count, head_size, state_width), jnp.float32),
    )
    neutral = running
    inside = []
    for counter in range(stretch_count):
        inside.append(running)
        running = combine(running, (stretch_logs[:, counter], stretch_states[:, counter]))
    gathered = (
        lax.all_gather(running[0][None].astype(jnp.bfloat16), "row", axis=0, tiled=True).astype(
            jnp.float32
        ),
        lax.all_gather(running[1][None].astype(jnp.bfloat16), "row", axis=0, tiled=True).astype(
            jnp.float32
        ),
    )
    row_before = neutral
    block_sum = neutral
    for counter in range(row_count):
        member = (gathered[0][counter], gathered[1][counter])
        row_before = choose_pair(counter < row_place, combine(row_before, member), row_before)
        block_sum = combine(block_sum, member)
    head_share = head_count // row_count
    part_logs = lax.dynamic_slice_in_dim(block_sum[0], row_place * head_share, head_share, 1)
    part_states = lax.dynamic_slice_in_dim(block_sum[1], row_place * head_share, head_share, 1)
    part_before = carried_in(
        (part_logs, part_states),
        COL,
        combine,
        (jnp.zeros_like(part_logs), jnp.zeros_like(part_states)),
    )
    col_state = gathered_copies(part_before[1], "row", 1)
    carry_in = jnp.exp(-row_before[0])[..., None, None] * col_state + row_before[1]
    entering = jnp.stack(
        [jnp.exp(-pair[0])[..., None, None] * carry_in + pair[1] for pair in inside], axis=1
    ).astype(jnp.bfloat16)
    carried_out = (
        jnp.einsum(
            "scqn,schpn->scqhp", outward_stretches, entering, preferred_element_type=jnp.float32
        )
        * jnp.exp(-log_decay)[..., None]
    )
    mixture = (local_out + carried_out).reshape(users, events, inner_width)
    gated_rows = mixture * jax.nn.silu(gate_rows.astype(jnp.float32))
    normed = (
        gated_rows
        * lax.rsqrt(jnp.mean(gated_rows * gated_rows, axis=-1, keepdims=True) + 1.0)
        * norm_gain
    ).astype(jnp.bfloat16)
    result = jnp.dot(
        normed.reshape(users * events, inner_width), w_out, preferred_element_type=jnp.float32
    ).reshape(users, events, -1)
    result = result * usable[..., None]
    return result.astype(jnp.bfloat16)[:, None]


def solution(mesh):
    split = Mesh(
        mesh.devices.reshape(mesh.shape["row"], 4, 8, mesh.shape["batch"]),
        ("row", "col_0", "col_1", "batch"),
    )
    in_specs = (
        P("batch", COL, "row"),
        P("batch", COL, "row"),
        P("batch"),
        P(),
        P(),
        P(),
        P(),
        P(),
        P(),
        P(),
        P(),
        P(),
    )
    out_specs = P("batch", COL, "row", None)
    return jax.shard_map(
        per_device, mesh=split, in_specs=in_specs, out_specs=out_specs, check_vma=False
    )
```

profile of v0, /device:TPU:8, one launch (start us, length us, event | category | flops | bytes accessed | tf_op | source)
XLA Modules:
  0.0 213.0 jit_solution(8130753456294840390)
XLA Ops:
  6.5 0.8 compare_select_fusion.1
  7.4 0.7 compare_and_fusion.1
  8.1 7.4 %gather_fusion = bf16[1024,1024]{1,0:T(8,128)(2,1)} fusion(bf16[512,1024]{1,0:T(8,128)(2,1)} %param.15, s32[1024]{0:T(1024)S(1)} %broadcast_clamp_fusion), kind=kCustom, calls=%fused_computation | custom fusion | bytes 4198400 | tf_op jit(solution)/shard_map/jit(_take)/gather | solution.py:98
  15.5 4.6 %convolution_convert_fusion = bf16[1024,1280]{1,0:T(8,128)(2,1)S(1)} fusion(bf16[1024,1280]{1,0:T(8,128)(2,1)S(1)} %copy-done, bf16[1024,1024]{1,0:T(8,128)(2,1)} %gather_fusion, pred[1024]{0:T(1024)(128)(4,1)S(1)} %compare_and_fusion.1), kind=kOutput, calls=%fused_computation.18 | convolution fusion | flops 2686713856 | bytes 7341056 | tf_op jit(solution)/shard_map/dot_general | solution.py:100
  20.1 1.5 copy-done.7
  21.6 1.6 collective-permute-start
  23.2 0.1 fusion.63
  23.3 2.3 %fusion.59 = f32[2,512,8]{1,2,0:T(8,128)S(1)} fusion(bf16[2,512,1024]{2,1,0:T(8,128)(2,1)} %bitcast.308, pred[2,512]{1,0:T(4,128)(4,1)S(1)} %get-tuple-element.57, bf16[1024,8]{0,1:T(8,128)(2,1)S(1)} %copy-done.16, f32[8]{0:T(128)S(1)} %copy-done.17, f32[2,512]{1,0:T(2,128)S(1)} %get-tuple-element.56), kind=kOutput, calls=%fused_computation.109 | convolution fusion | flops 17891328 | bytes 2151456 | tf_op jit(solution)/shard_map/dot_general | solution.py:109
  25.7 0.1 multiply_bitcast_fusion
  25.7 0.2 copy.74
  25.9 0.5 reduce_window_sum.11
  26.4 0.2 copy.75
  26.6 0.2 slice_reduce_fusion
  26.8 0.1 exponential_multiply_fusion
  26.9 3.8 %collective-permute-start.1 = (bf16[2,3,1280]{2,1,0:T(4,128)(2,1)S(1)}, bf16[2,3,1280]{2,1,0:T(4,128)(2,1)S(1)}, u32[]{:S(2)}, u32[]{:S(2)}) collective-permute-start(bf16[2,3,1280]{2,1,0:T(4,128)(2,1)S(1)} %collective-permute-done), channel_id=1, source_target_pairs={{0,2},{2,4},{4,6},{6,8},{8,10},{10,12},{12,14},{14,16},{16,18},{18... | collective-permute-start | bytes 46088 | tf_op jit(solution)/shard_map/ppermute | solution.py:20
  30.8 0.1 slice_reduce_fusion.4
  30.8 5.5 %collective-permute-done.1 = bf16[2,3,1280]{2,1,0:T(4,128)(2,1)S(1)} collective-permute-done((bf16[2,3,1280]{2,1,0:T(4,128)(2,1)S(1)}, bf16[2,3,1280]{2,1,0:T(4,128)(2,1)S(1)}, u32[]{:S(2)}, u32[]{:S(2)}) %collective-permute-start.1) | collective-permute-done | bytes 15392 | tf_op jit(solution)/shard_map/ppermute | solution.py:20
  36.3 6.2 %fusion.84 = (bf16[2,512,1280]{2,1,0:T(8,128)(2,1)S(1)}, f32[2,512,1280]{2,1,0:T(8,128)S(1)}) fusion(f32[1280]{0:T(1024)S(1)} %get-tuple-element.7, bf16[2,512,1280]{2,1,0:T(8,128)(2,1)} %bitcast.305, f32[1280]{0:T(1024)S(1)} %get-tuple-element.8, bf16[2,3,1280]{2,1,0:T(4,128)(2,1)S(1)} %select_select_fusion, f32[1280]{0:T(1024)S(1)} %get-tuple-element.6, ...), kind=kLoop, calls=%fused_computation.195 | loop fusion | flops 27525120 | bytes 10521600 | tf_op jit(solution)/shard_map/convert.6
  42.6 0.8 fusion.85
  43.4 1.1 multiply_convert_fusion.3
  44.5 2.0 copy.94
  46.5 3.2 %copy.76 = bf16[2,4,128,8,128]{2,4,3,1,0:T(8,128)(2,1)S(1)} copy(bf16[2,4,128,8,128]{4,3,2,1,0:T(8,128)(2,1)} %bitcast.302) | data formatting | bytes 4194304 | tf_op jit(solution)/shard_map/reshape | solution.py:139
  49.7 2.3 %fusion.10 = f32[2,4,8,128,128]{4,3,2,1,0:T(8,128)S(1)} fusion(bf16[2,4,128,8,128]{2,4,3,1,0:T(8,128)(2,1)S(1)} %copy.76, f32[2,4,8,128]{3,2,1,0:T(8,128)S(1)} %exponential_multiply_fusion, f32[2,4,128,128]{3,2,1,0:T(8,128)S(1)} %convert_element_type.104), kind=kOutput, calls=%fused_computation.25 | convolution fusion | flops 270532608 | bytes 6848512 | tf_op jit(solution)/shard_map/schun,scuhp->schpn/dot_general | solution.py:156
  52.0 1.9 copy-done.3
  53.9 1.3 fusion.31
  55.2 0.0 all-gather.8.cloned.1.call-update
  55.2 0.0 all-gather.12.cloned.1.call-start
  55.3 8.7 %all-gather = bf16[8,1,8]{2,1,0:T(2,128)(2,1)S(1)} all-gather(bf16[2,1,8]{2,1,0:T(2,128)(2,1)S(1)} %get-tuple-element.35), channel_id=2, replica_groups=mesh['row'=4,'col_0'=4,'col_1'=8,'batch'=2] {'row'}, dimensions={0}, use_global_device_ids=true | all-gather | bytes 160 | tf_op jit(solution)/shard_map/all_gather | solution.py:170
  64.0 0.1 constant_dynamic-slice_fusion
  64.1 0.1 constant_dynamic-slice_fusion.1
  64.2 0.1 constant_dynamic-slice_fusion.2
  64.2 24.5 %all-gather.8.cloned.1.call-done = bf16[4,2,8,128,128]{4,3,2,1,0:T(8,128)(2,1)} async-done(((bf16[1,2,8,128,128]{4,3,2,1,0:T(8,128)(2,1)}), bf16[4,2,8,128,128]{4,3,2,1,0:T(8,128)(2,1)}) %all-gather.8.cloned.1.call-update) | async-done | bytes 2097168 | tf_op jit(solution)/shard_map/all_gather | solution.py:173
  88.8 2.1 convert_element_type.107
  90.9 0.3 slice_bitcast_fusion.3
  91.2 0.1 bitcast_add_fusion.11
  91.3 1.6 copy-done.2
  92.9 0.8 dynamic-slice_add_fusion
  93.8 0.0 all-gather.10.cloned.1.call-start
  93.8 0.1 fusion.64
  93.9 16.7 %all-gather.3 = f32[8,2,2]{2,1,0:T(2,128)S(1)} all-gather(f32[1,2,2]{2,1,0:T(2,128)S(1)} %fusion.64), channel_id=3, replica_groups=mesh['row'=4,'col_0'=4,'col_1'=8,'batch'=2] {'col_1'}, dimensions={0}, use_global_device_ids=true | all-gather | bytes 144 | tf_op jit(solution)/shard_map/all_gather | solution.py:34
  110.6 24.2 %all-gather.12.cloned.1.call-done = f32[16,2,128,128]{3,2,1,0:T(8,128)} async-done(((f32[2,2,128,128]{3,2,1,0:T(8,128)}), f32[16,2,128,128]{3,2,1,0:T(8,128)}) %all-gather.12.cloned.1.call-update) | async-done | bytes 2097168 | tf_op jit(solution)/shard_map/all_gather | solution.py:34
  134.8 2.4 %bitcast_add_fusion.12 = f32[1,2,2,128,128]{4,3,2,1,0:T(8,128)} fusion(f32[16,2,128,128]{3,2,1,0:T(8,128)} %all-gather.12.cloned.1.call-done, f32[2,2]{1,0:T(2,128)S(1)} %get-tuple-element.33, f32[2,2]{1,0:T(2,128)S(1)} %get-tuple-element.32, f32[2,2]{1,0:T(2,128)S(1)} %get-tuple-element.30, f32[2,2]{1,0:T(2,128)S(1)} %get-tuple-element.27, ...), kind=kLoop, calls=%fused_computation.92 | loop fusion | flops 983040 | bytes 2359424 | tf_op jit(solution)/shard_map/add | solution.py:61
  137.3 8.0 %all_gather.29 = f32[4,2,2]{2,1,0:T(2,128)S(1)} all-gather(f32[1,2,2]{2,1,0:T(2,128)S(1)} %get-tuple-element.14), channel_id=1, replica_groups=mesh['row'=4,'col_0'=4,'col_1'=8,'batch'=2] {'col_0'}, dimensions={0}, use_global_device_ids=true | all-gather | bytes 80 | tf_op jit(solution)/shard_map/all_gather | solution.py:34
  145.3 0.1 negate_exponential_fusion
  145.4 0.2 copy.83
  145.6 4.7 %convolution_convert_fusion.1 = bf16[1024,1024]{1,0:T(8,128)(2,1)S(1)} fusion(bf16[1024,1024]{1,0:T(8,128)(2,1)} %param.16, bf16[1024,1024]{1,0:T(8,128)(2,1)} %gather_fusion, pred[1024]{0:T(1024)(128)(4,1)S(1)} %compare_and_fusion.1), kind=kOutput, calls=%fused_computation.41 | convolution fusion | flops 2149580800 | bytes 6292480 | tf_op jit(solution)/shard_map/dot_general | solution.py:105
  150.2 0.5 convert_bitcast_fusion
  150.7 3.0 %copy.96 = f32[128,8,8,128]{3,2,1,0:T(8,128)} copy(f32[128,8,8,128]{3,1,2,0:T(8,128)S(1)} %convert_bitcast_fusion) | data formatting | bytes 8388608
  153.7 5.3 %copy.86 = f32[2,4,128,8,128]{2,4,3,1,0:T(8,128)} copy(f32[2,4,128,8,128]{4,3,2,1,0:T(8,128)} %bitcast.300) | data formatting | bytes 8388608 | tf_op jit(solution)/shard_map/convert_element_type | solution.py:204
  159.0 2.5 %all-gather.10.cloned.1.call-done = f32[4,2,2,128,128]{4,3,2,1,0:T(8,128)} async-done(((f32[1,2,2,128,128]{4,3,2,1,0:T(8,128)}), f32[4,2,2,128,128]{4,3,2,1,0:T(8,128)}) %all-gather.10.cloned.1.call-update) | async-done | bytes 1048592 | tf_op jit(solution)/shard_map/all_gather | solution.py:34
  161.5 2.3 %fusion.46 = f32[2,2,128,128]{3,2,1,0:T(8,128)S(1)} fusion(f32[4,2,2,128,128]{4,3,2,1,0:T(8,128)} %all-gather.10.cloned.1.call-done, f32[16,2,128,128]{3,2,1,0:T(8,128)} %all-gather.12.cloned.1.call-done, f32[2,2]{1,0:T(2,128)S(1)} %get-tuple-element.30, f32[2,2]{1,0:T(2,128)S(1)} %get-tuple-element.29, f32[2,2]{1,0:T(2,128)S(1)} %get-tuple-element.27, ...), kind=kLoop, calls=%fused_computation.79 | loop fusion | flops 2359296 | bytes 3408092 | tf_op jit(solution)/shard_map/add | solution.py:61
  163.8 1.1 broadcast_in_dim.44
  164.9 4.2 %all-to-all-start = ((f32[4,2,2,128,128]{4,3,2,1,0:T(8,128)}), f32[4,2,2,128,128]{4,3,2,1,0:T(8,128)}, u32[]{:S(2)}, u32[]{:S(2)}) async-start(f32[4,2,2,128,128]{4,3,2,1,0:T(8,128)} %broadcast_in_dim.44), calls=%async_computation | async-start | bytes 2097152 | tf_op jit(solution)/shard_map/all_to_all | solution.py:46
  169.2 0.3 fusion.87
  169.5 4.4 %fusion.9 = f32[2,4,8,128,128]{4,3,2,1,0:T(8,128)} fusion(bf16[2,4,128,8,128]{2,4,3,1,0:T(8,128)(2,1)} %copy-done.5, f32[2,4,8,128]{3,2,1,0:T(8,128)S(1)} %bitcast.314, f32[2,4,8,128]{3,2,1,0:T(8,128)S(1)} %bitcast.313, f32[2,4,128,128]{3,2,1,0:T(8,128)S(1)} %fusion.87, pred[128,128]{1,0:T(8,128)(4,1)S(1)} %iota_compare_fusion), kind=kOutput, calls=%fused_computation.24 | convolution fusion | flops 275775488 | bytes 6897664 | tf_op jit(solution)/shard_map/schqu,scuhp->scqhp/dot_general | solution.py:151
  173.9 9.1 %all-to-all-done = f32[4,2,2,128,128]{4,3,2,1,0:T(8,128)} async-done(((f32[4,2,2,128,128]{4,3,2,1,0:T(8,128)}), f32[4,2,2,128,128]{4,3,2,1,0:T(8,128)}, u32[]{:S(2)}, u32[]{:S(2)}) %all-to-all-start) | async-done | bytes 1048608 | tf_op jit(solution)/shard_map/all_to_all | solution.py:46
  183.0 1.4 copy.81
  184.4 3.5 %fusion.82 = (bf16[2,1,8,128,128]{4,3,2,0,1:T(8,128)(2,1)S(1)}, f32[2,1,8,128,128]{4,3,2,0,1:T(8,128)S(1)}) fusion(f32[4,2,8,128,128]{4,3,2,1,0:T(8,128)} %copy-done.2, f32[2,8]{1,0:T(2,128)S(1)} %get-tuple-element.50, pred[]{:T(512)S(6)} %gt.64, f32[2,8]{1,0:T(2,128)S(1)} %get-tuple-element.51, pred[]{:T(512)S(6)} %gt.63, ...), kind=kLoop, calls=%fused_computation.194 | loop fusion | flops 3670016 | bytes 6816068 | tf_op jit(solution)/shard_map/convert.1
  188.0 0.7 add_convert_fusion
  188.8 1.5 copy-done.6
  190.2 3.1 %multiply_reduce_fusion = (f32[2,4,128]{2,1,0:T(4,128)S(1)}, f32[2,4,128,8,128]{2,4,3,1,0:T(8,128)}) fusion(f32[2,4,128,8,128]{2,4,3,1,0:T(8,128)S(1)} %copy-done.6, f32[2,4,128,8]{2,3,1,0:T(8,128)S(1)} %copy.83, bf16[2,4,128,128,1]{3,2,4,1,0:T(8,128)(2,1)S(1)} %bitcast.311, f32[2,4,8,128,128]{4,3,2,1,0:T(8,128)S(1)} %copy-done.18, ...), kind=kOutput, calls=%fused_computation.13 | convolution fusion | flops 281017344 | bytes 14979072 | tf_op jit(solution)/shard_map/scqn,schpn->scqhp/dot_general | solution.py:198
  193.3 5.3 %copy.84 = f32[2,4,128,8,128]{4,3,2,1,0:T(8,128)} copy(f32[2,4,128,8,128]{2,4,3,1,0:T(8,128)} %get-tuple-element.55) | data formatting | bytes 8388608 | tf_op jit(solution)/shard_map/add | solution.py:203
  198.6 4.1 %fusion.6 = bf16[1024,1024]{1,0:T(8,128)(2,1)S(1)} fusion(bf16[1024,1024]{1,0:T(8,128)(2,1)S(1)} %convolution_convert_fusion.1, f32[128,8,8,128]{3,2,1,0:T(8,128)} %bitcast.299, f32[1024]{0:T(1024)S(1)} %copy-done.11, f32[1024]{0:T(1024)S(1)} %bitcast.316), kind=kLoop, calls=%fused_computation.17 | loop fusion | flops 9437184 | bytes 8396800 | tf_op jit(solution)/shard_map/convert_element_type | solution.py:209
  202.8 3.7 %fusion.24 = bf16[2,1,512,1024]{3,2,1,0:T(8,128)(2,1)} fusion(f32[2,512]{1,0:T(2,128)S(1)} %get-tuple-element.56, bf16[2,512,1024]{2,1,0:T(8,128)(2,1)S(1)} %bitcast.309, bf16[1024,1024]{1,0:T(8,128)(2,1)S(1)} %copy-done.15), kind=kOutput, calls=%fused_computation.42 | convolution fusion | flops 2149580800 | bytes 6295552 | tf_op jit(solution)/shard_map/dot_general | solution.py:210
  (55 shorter events, 0.3 us)
Async XLA Ops:
  6.5 8.9 %copy-start = (bf16[1024,1280]{1,0:T(8,128)(2,1)S(1)}, bf16[1024,1280]{1,0:T(8,128)(2,1)}, u32[]{:S(2)}) copy-start(bf16[1024,1280]{1,0:T(8,128)(2,1)} %param.17) | copy-start | bytes 7864324
  6.5 82.2 %all-gather.8.cloned.1.call-start = ((), (), s32[]{:S(2)}) async-start(), calls=%async_computation.1 | async-start | bytes 2621440 | tf_op jit(solution)/shard_map/all_gather | solution.py:173
  15.5 7.7 %copy-start.12 = (s32[2,1,512]{2,1,0:T(1,128)S(1)}, s32[2,1,512]{2,1,0:T(1,128)}, u32[]{:S(2)}) copy-start(s32[2,1,512]{2,1,0:T(1,128)} %param.13) | copy-start | bytes 12292
  15.5 7.7 %copy-start.9 = (s32[2,1,512]{2,1,0:T(1,128)S(1)}, s32[2,1,512]{2,1,0:T(1,128)}, u32[]{:S(2)}) copy-start(s32[2,1,512]{2,1,0:T(1,128)} %param.12) | copy-start | bytes 12292
  15.5 7.7 %copy-start.14 = (s32[2]{0:T(128)S(1)}, s32[2]{0:T(128)}, u32[]{:S(2)}) copy-start(s32[2]{0:T(128)} %param.14) | copy-start | bytes 28
  15.5 7.8 %copy-start.16 = (bf16[1024,8]{0,1:T(8,128)(2,1)S(1)}, bf16[1024,8]{0,1:T(8,128)(2,1)}, u32[]{:S(2)}) copy-start(bf16[1024,8]{0,1:T(8,128)(2,1)} %param.18) | copy-start | bytes 49156
  15.5 7.8 %copy-start.17 = (f32[8]{0:T(128)S(1)}, f32[8]{0:T(128)}, u32[]{:S(2)}) copy-start(f32[8]{0:T(128)} %param.20) | copy-start | bytes 100
  15.5 10.1 %copy-start.13 = (f32[8]{0:T(128)S(1)}, f32[8]{0:T(128)}, u32[]{:S(2)}) copy-start(f32[8]{0:T(128)} %param.21) | copy-start | bytes 100
  20.1 1.5 copy-start.7
  20.1 10.7 %copy-start.10 = (f32[4,1280]{1,0:T(4,128)S(1)}, f32[4,1280]{1,0:T(4,128)}, u32[]{:S(2)}) copy-start(f32[4,1280]{1,0:T(4,128)} %param.19) | copy-start | bytes 61444
  21.6 5.3 %collective-permute-start = (bf16[2,3,1280]{2,1,0:T(4,128)(2,1)S(1)}, bf16[2,3,1280]{2,1,0:T(4,128)(2,1)S(1)}, u32[]{:S(2)}, u32[]{:S(2)}) collective-permute-start(bf16[2,3,1280]{2,1,0:T(4,128)(2,1)S(1)} %slice.241), channel_id=1, source_target_pairs={{192,0},{0,64},{64,128},{128,192},{193,1},{1,65},{65,129},{129,193... | collective-permute-start | bytes 46088 | tf_op jit(solution)/shard_map/ppermute | solution.py:14
  26.9 9.4 %collective-permute-start.1 = (bf16[2,3,1280]{2,1,0:T(4,128)(2,1)S(1)}, bf16[2,3,1280]{2,1,0:T(4,128)(2,1)S(1)}, u32[]{:S(2)}, u32[]{:S(2)}) collective-permute-start(bf16[2,3,1280]{2,1,0:T(4,128)(2,1)S(1)} %collective-permute-done), channel_id=1, source_target_pairs={{0,2},{2,4},{4,6},{6,8},{8,10},{10,12},{12,14},{14,16},{16,18},{18... | collective-permute-start | bytes 46088 | tf_op jit(solution)/shard_map/ppermute | solution.py:20
  49.7 5.5 %copy-start.5 = (bf16[2,4,128,8,128]{2,4,3,1,0:T(8,128)(2,1)}, bf16[2,4,128,8,128]{2,4,3,1,0:T(8,128)(2,1)S(1)}, u32[]{:S(2)}) copy-start(bf16[2,4,128,8,128]{2,4,3,1,0:T(8,128)(2,1)S(1)} %copy.76) | copy-start | bytes 6291460
  52.0 2.0 copy-start.3
  55.2 79.6 %all-gather.12.cloned.1.call-start = ((), (), s32[]{:S(2)}) async-start(), calls=%async_computation.3 | async-start | bytes 2359296 | tf_op jit(solution)/shard_map/all_gather | solution.py:34
  90.9 2.0 copy-start.2
  93.8 67.7 %all-gather.10.cloned.1.call-start = ((), (), s32[]{:S(2)}) async-start(), calls=%async_computation.2 | async-start | bytes 1310720 | tf_op jit(solution)/shard_map/all_gather | solution.py:34
  159.0 10.2 %copy-start.8 = (bf16[2,512,128]{2,1,0:T(8,128)(2,1)S(1)}, bf16[2,512,128]{2,1,0:T(8,128)(2,1)}, u32[]{:S(2)}) copy-start(bf16[2,512,128]{2,1,0:T(8,128)(2,1)} %get-tuple-element.24) | copy-start | bytes 786436
  164.9 18.1 %all-to-all-start = ((f32[4,2,2,128,128]{4,3,2,1,0:T(8,128)}), f32[4,2,2,128,128]{4,3,2,1,0:T(8,128)}, u32[]{:S(2)}, u32[]{:S(2)}) async-start(f32[4,2,2,128,128]{4,3,2,1,0:T(8,128)} %broadcast_in_dim.44), calls=%async_computation | async-start | bytes 2097152 | tf_op jit(solution)/shard_map/all_to_all | solution.py:46
  183.0 5.0 %copy-start.4 = (f32[2,4,8,128,128]{4,3,2,1,0:T(8,128)S(1)}, f32[2,4,8,128,128]{4,3,2,1,0:T(8,128)}, u32[]{:S(2)}) copy-start(f32[2,4,8,128,128]{4,3,2,1,0:T(8,128)} %copy-done.3) | copy-start | bytes 12582916
  184.4 4.3 %copy-start.18 = (f32[2,4,8,128,128]{4,3,2,1,0:T(8,128)S(1)}, f32[2,4,8,128,128]{4,3,2,1,0:T(8,128)}, u32[]{:S(2)}) copy-start(f32[2,4,8,128,128]{4,3,2,1,0:T(8,128)} %fusion.9) | copy-start | bytes 12582916
  188.0 2.3 %copy-start.6 = (f32[2,4,128,8,128]{2,4,3,1,0:T(8,128)S(1)}, f32[2,4,128,8,128]{2,4,3,1,0:T(8,128)}, u32[]{:S(2)}) copy-start(f32[2,4,128,8,128]{2,4,3,1,0:T(8,128)} %copy.86) | copy-start | bytes 12582916
  193.3 5.4 %copy-start.11 = (f32[1024]{0:T(1024)S(1)}, f32[1024]{0:T(1024)}, u32[]{:S(2)}) copy-start(f32[1024]{0:T(1024)} %param.22) | copy-start | bytes 12292
  198.6 4.2 %copy-start.15 = (bf16[1024,1024]{1,0:T(8,128)(2,1)S(1)}, bf16[1024,1024]{1,0:T(8,128)(2,1)}, u32[]{:S(2)}) copy-start(bf16[1024,1024]{1,0:T(8,128)(2,1)} %param.23) | copy-start | bytes 6291460
  202.8 3.7 %copy-start.1 = (bf16[1024,1280]{1,0:T(8,128)(2,1)S(1)}, bf16[1024,1280]{1,0:T(8,128)(2,1)}, u32[]{:S(2)}) copy-start(bf16[1024,1280]{1,0:T(8,128)(2,1)} %param.17) | copy-start | bytes 7864324
Sparse Core Ops, SparseCore 0:
  55.4 33.3 all-gather.7
  93.9 40.9 all-gather.11
  137.4 24.0 all-gather.9
where the time goes:
time: 214 us; the launch traced here: 213 us
  waiting for transfers between devices  65.8 us (31%)
  local copies, waits for them, and re-layouts  37.4 us (17%)
  blocking collectives  33.4 us (16%)
  other arithmetic  27.8 us (13%)
  matrix products  25.3 us (12%)
  between operations  13.6 us (6%)
  starting transfers between devices  9.73 us (5%)
    all_gather x2, waiting for transfers between devices, carried_in(): pieces = jax.tree.map(lambda part: lax.all_gather(part, axis), subtotal)  26.7 us
    all_gather x2, blocking collectives, carried_in(): pieces = jax.tree.map(lambda part: lax.all_gather(part, axis), subtotal)  24.7 us
    all_gather x1, waiting for transfers between devices, per_device(): lax.all_gather(running[1][None].astype(jnp.bfloat16), 'row', axis=0, tile...  24.5 us
    unnamed x41, local copies, waits for them, and re-layouts  11.6 us
    another operation x3, other arithmetic  10.5 us
    all_to_all x1, waiting for transfers between devices, copy_for_each(): return lax.all_to_all(copies, axis, split_axis=0, concat_axis=0, tiled=True)  9.05 us
    all_gather x1, blocking collectives, per_device(): lax.all_gather(running[0][None].astype(jnp.bfloat16), 'row', axis=0, tile...  8.72 us
    gather x1, local copies, waits for them, and re-layouts, per_device(): jnp.take(item_table, item_rows, axis=0).reshape(users * events, -1)  7.37 us
  transfers between devices with their start and end apart: 6, of which 5 were waited for; matrix products, arithmetic and copies ran while one was open for 11% of the time, Pallas kernels for 0%

commit v1 on v0

v1 whole, which is shorter than its diff:
```python
import functools

import jax
import jax.numpy as jnp
from jax import lax
from jax.experimental import pallas as pl
from jax.experimental.pallas import tpu as pltpu
from jax.sharding import PartitionSpec as P

STRETCH = 128
CHUNK = 256
HALO = 16
ROWS, YS, ZS = 4, 4, 8
MESH = pl.DeviceIdType.MESH
BF16 = jnp.bfloat16
F32 = jnp.float32


def silu(v):
    return v * (0.5 * jnp.tanh(0.5 * v) + 0.5)


def dot(a, b):
    return jnp.dot(a, b, preferred_element_type=F32)


def down_columns(row):
    return jnp.transpose(jnp.broadcast_to(row, (STRETCH, STRETCH)))


def local_kernel(
    lengths,
    ids,
    halo,
    pads,
    table,
    w_gate,
    w_in,
    w_dt,
    taps,
    bias,
    rates,
    state_out,
    logs_out,
    mix,
    gate,
    outward,
    decays,
    wdt_wide,
    bias_wide,
    rates_wide,
    hot,
    joined,
    signal,
    inward,
    steps,
    running,
    passed,
):
    users, _, events = ids.shape
    inner = w_gate.shape[1]
    heads = w_dt.shape[1]
    stretches = events // STRETCH
    first = (lax.axis_index("col") * ROWS + lax.axis_index("row")) * events
    lanes = lax.broadcasted_iota(jnp.int32, (STRETCH, STRETCH), 1)
    lanes_f = lanes.astype(F32)

    def one_hot(row, place, rows):
        column = down_columns(row)[STRETCH - rows :, :]
        for j in range(table.shape[0] // STRETCH):
            match = column == lanes_f[:rows] + float(j * STRETCH)
            hot[place[0], pl.ds(place[1], rows), j * STRETCH : (j + 1) * STRETCH] = jnp.where(
                match, 1.0, 0.0
            ).astype(BF16)

    for u in range(users):
        one_hot(halo[u].astype(F32) - 1.0, (u, 0), HALO)
        for c in range(stretches):
            one_hot(
                ids[u, :, c * STRETCH : (c + 1) * STRETCH].astype(F32),
                (u, HALO + c * STRETCH),
                STRETCH,
            )

    wdt_wide[...] = jnp.zeros_like(wdt_wide)
    wdt_wide[:, 0:heads] = w_dt[...]
    bias_wide[...] = jnp.zeros_like(bias_wide)
    bias_wide[:, 0:heads] = bias[...]
    rates_wide[...] = jnp.zeros_like(rates_wide)
    rates_wide[:, 0:heads] = rates[...]
    raw = dot(table[...], wdt_wide[...]) + bias_wide[...]
    soft = jnp.maximum(raw, 0.0) + jnp.log1p(jnp.exp(-jnp.abs(raw)))
    high = soft.astype(BF16)
    rest = soft - high.astype(F32)
    middle = rest.astype(BF16)
    low = (rest - middle.astype(F32)).astype(BF16)
    for u in range(users):
        picks = hot[u, HALO:, :]
        step = dot(picks, high) + (dot(picks, middle) + dot(picks, low))
        for c in range(stretches):
            place = first + c * STRETCH + lax.broadcasted_iota(jnp.int32, (1, STRETCH), 1)
            kept = jnp.logical_and(
                place < lengths[u], pads[u, :, c * STRETCH : (c + 1) * STRETCH] > 0
            )
            usable = down_columns(jnp.where(kept, 1.0, 0.0))
            rows = slice(c * STRETCH, (c + 1) * STRETCH)
            steps[u, rows, :] = jnp.where(
                lanes == heads, usable, jnp.where(lanes < heads, step[rows] * usable, 0.0)
            )

    def project(j, weights):
        columns = pl.ds(pl.multiple_of(j * CHUNK, CHUNK), CHUNK)
        return columns, dot(table[...], weights[:, columns]).astype(BF16)

    def convolve(columns, projected, u):
        joined[u] = dot(hot[u], projected)
        total = None
        for k in range(taps.shape[0]):
            begin = HALO - taps.shape[0] + 1 + k
            term = joined[u, begin : begin + events, :] * taps[k : k + 1, columns]
            total = term if total is None else total + term
        return total

    @pl.loop(0, inner // CHUNK)
    def _(j):
        columns, projected = project(j, w_in)
        for u in range(users):
            signal[u, :, columns] = silu(convolve(columns, projected, u)).astype(BF16)
        columns, projected = project(j, w_gate)
        opened = silu(projected.astype(F32)).astype(BF16)
        for u in range(users):
            gate[u, :, columns] = dot(hot[u, HALO:, :], opened).astype(BF16)

    columns, projected = project(inner // CHUNK, w_in)
    for u in range(users):
        maps = convolve(columns, projected, u).astype(BF16)
        inward[u] = maps[:, 0:STRETCH]
        outward[u] = maps[:, STRETCH:]

    causal = lax.broadcasted_iota(jnp.int32, (STRETCH, STRETCH), 0) >= lanes
    lower = jnp.where(causal, 1.0, 0.0)
    running[...] = jnp.zeros_like(running)
    passed[...] = jnp.zeros_like(passed)

    @pl.loop(0, users * stretches)
    def _(s):
        u = s // stretches
        c = lax.rem(s, stretches)
        rows = pl.ds(pl.multiple_of(c * STRETCH, STRETCH), STRETCH)
        opening = c == 0
        step = steps[u, rows, :]
        log = jnp.dot(
            lower,
            step * rates_wide[...],
            preferred_element_type=F32,
            precision=lax.Precision.HIGHEST,
        )
        before = jnp.where(opening, 0.0, passed[...])
        decays[u, rows, :] = jnp.where(lanes == heads, step, jnp.exp(-(log + before)))
        passed[...] = before + log[STRETCH - 1 :, :]
        fade = jnp.exp(-log)
        log_t = jnp.transpose(log)[0:heads]
        step_t = jnp.transpose(step)[0:heads]
        last = log_t[:, STRETCH - 1 :]
        tail_t = jnp.exp(log_t - last) * step_t
        stay = jnp.exp(-last)
        ins = inward[u, rows, :]
        outs = outward[u, rows, :]
        in_t = jnp.transpose(ins.astype(F32))
        scores = lax.dot_general(outs, ins, (((1,), (1,)), ((), ())), preferred_element_type=F32)
        for h in range(heads):
            cols = slice(h * STRETCH, (h + 1) * STRETCH)
            inside = jnp.where(opening, 0.0, running[:, cols])
            gap = jnp.where(causal, log_t[h : h + 1, :] - log[:, h : h + 1], -1e30)
            weights = (scores * jnp.exp(gap) * step_t[h : h + 1, :]).astype(BF16)
            values = signal[u, rows, cols]
            mix[u, rows, cols] = (
                dot(weights, values) + dot(outs, inside.astype(BF16)) * fade[:, h : h + 1]
            ).astype(BF16)
            scaled = (in_t * tail_t[h : h + 1, :]).astype(BF16)
            running[:, cols] = stay[h : h + 1, :] * inside + dot(scaled, values)

        @pl.when(c == stretches - 1)
        def _():
            for h in range(heads):
                r, half = h // 2, h % 2
                cols = slice(half * STRETCH, (half + 1) * STRETCH)
                state_out[r, u, :, cols] = running[:, h * STRETCH : (h + 1) * STRETCH].astype(BF16)
                logs_out[r, u, :, cols] = jnp.broadcast_to(passed[:, h : h + 1], (1, STRETCH))


def scan_kernel(
    states,
    logs,
    carry,
    row_states,
    row_logs,
    row_before,
    z_out,
    z_states,
    z_log_out,
    z_logs,
    y_out,
    y_states,
    y_log_out,
    y_logs,
    c_out,
    c_states,
    back_out,
    x_send,
    x_recv,
    xl_send,
    xl_recv,
    z_send,
    z_recv,
    zl_send,
    zl_recv,
    y_send,
    y_recv,
    yl_send,
    yl_recv,
    c_send,
    c_recv,
    b_send,
    b_recv,
):
    users = states.shape[1]
    part = z_states.shape[2]
    r = lax.axis_index("row")
    col = lax.axis_index("col")
    y, z = col // ZS, lax.rem(col, ZS)

    def row_peer(d):
        return lax.rem(r + d, ROWS)

    def z_peer(d):
        return lax.rem(z + d, ZS)

    def y_peer(d):
        return lax.rem(y + d, YS)

    def to_row(d):
        return {"row": row_peer(d)}

    def to_z(d):
        return {"col": y * ZS + z_peer(d)}

    def to_y(d):
        return {"col": y_peer(d) * ZS + z}

    barrier = pltpu.get_barrier_semaphore()
    peers = (
        [to_row(d) for d in range(1, ROWS)]
        + [to_z(d) for d in range(1, ZS)]
        + [to_y(d) for d in range(1, YS)]
    )
    for peer in peers:
        pl.semaphore_signal(barrier, inc=1, device_id=peer, device_id_type=MESH)
    pl.semaphore_wait(barrier, len(peers))

    sent = []

    def send(src, dst, send_sem, recv_sem, device):
        copy = pltpu.make_async_remote_copy(
            src_ref=src,
            dst_ref=dst,
            send_sem=send_sem,
            recv_sem=recv_sem,
            device_id=device,
            device_id_type=MESH,
        )
        copy.start()
        sent.append(copy)
        return copy

    x_copies, xl_copies = {}, {}
    for d in (2, 1, 3):
        xl_copies[d] = send(
            logs.at[row_peer(d)], row_logs.at[r], xl_send.at[d], xl_recv.at[d], to_row(d)
        )
    for u in range(users):
        for d in (2, 1, 3):
            x_copies[u, d] = send(
                states.at[row_peer(d), u],
                row_states.at[u, r],
                x_send.at[u, d],
                x_recv.at[u, d],
                to_row(d),
            )
    row_logs[r] = logs[r]
    for u in range(users):
        row_states[u, r] = states[r, u]

    for d in range(1, ROWS):
        xl_copies[d].wait_recv()
    block_log = row_logs[0]
    for i in range(1, ROWS):
        block_log = block_log + row_logs[i]
    z_log_out[...] = block_log
    z_logs[z] = block_log
    zl_copies = [
        send(z_log_out, z_logs.at[z], zl_send.at[d], zl_recv.at[d], to_z(d)) for d in range(1, ZS)
    ]

    z_copies = {}
    for u in range(users):
        for d in range(1, ROWS):
            x_copies[u, d].wait_recv()
        total = row_states[u, 0].astype(F32)
        for i in range(1, ROWS):
            row_before[u, i - 1] = total
            total = jnp.exp(-row_logs[i, u]) * total + row_states[u, i].astype(F32)
        block = total.astype(BF16)
        for k in range(ZS):
            z_out[u, k] = block[k * part : (k + 1) * part]
        z_states[u, z] = z_out[u, z]
        for d in (4, 3, 5, 2, 6, 1, 7):
            z_copies[u, d] = send(
                z_out.at[u, z_peer(d)],
                z_states.at[u, z],
                z_send.at[u, d],
                z_recv.at[u, d],
                to_z(d),
            )

    for copy in zl_copies:
        copy.wait_recv()
    y_log = z_logs[0]
    for i in range(1, ZS):
        y_log = y_log + z_logs[i]
    y_log_out[...] = y_log
    y_logs[y] = y_log
    yl_copies = [
        send(y_log_out, y_logs.at[y], yl_send.at[d], yl_recv.at[d], to_y(d)) for d in range(1, YS)
    ]

    y_copies, z_before = {}, {}
    for u in range(users):
        for d in range(1, ZS):
            z_copies[u, d].wait_recv()
        z_before[u] = [None]
        total = z_states[u, 0].astype(F32)
        for i in range(1, ZS):
            z_before[u].append(total)
            total = jnp.exp(-z_logs[i, u]) * total + z_states[u, i].astype(F32)
        y_out[u] = total.astype(BF16)
        for d in (2, 1, 3):
            y_copies[u, d] = send(
                y_out.at[u], y_states.at[u, y], y_send.at[u, d], y_recv.at[u, d], to_y(d)
            )

    for copy in yl_copies:
        copy.wait_recv()
    c_copies = {}
    for u in range(users):
        for d in range(1, YS):
            y_copies[u, d].wait_recv()
        y_states[u, y] = jnp.zeros_like(y_states[u, y])
        entering = jnp.zeros(y_out.shape[1:], F32)
        for i in range(YS - 1):
            entering = jnp.where(
                i < y, jnp.exp(-y_logs[i, u]) * entering + y_states[u, i].astype(F32), entering
            )
        gone = None
        for k in range(ZS):
            value = entering
            if k:
                gone = z_logs[k - 1, u] if gone is None else gone + z_logs[k - 1, u]
                value = jnp.exp(-gone) * entering + z_before[u][k]
            c_out[u, k] = value.astype(BF16)
        c_states[u, z] = c_out[u, z]
        for d in (4, 3, 5, 2, 6, 1, 7):
            c_copies[u, d] = send(
                c_out.at[u, z_peer(d)],
                c_states.at[u, z],
                c_send.at[u, d],
                c_recv.at[u, d],
                to_z(d),
            )

    b_copies = {}
    for u in range(users):
        for d in range(1, ZS):
            c_copies[u, d].wait_recv()
        gone = None
        for i in range(ROWS):
            if i:
                gone = row_logs[i - 1, u] if gone is None else gone + row_logs[i - 1, u]
            for k in range(ZS):
                rows = slice(k * part, (k + 1) * part)
                value = c_states[u, k].astype(F32)
                if i:
                    value = jnp.exp(-gone) * value + row_before[u, i - 1, rows, :]
                back_out[u, i, rows, :] = value.astype(BF16)
        carry[u, r] = back_out[u, r]
        for d in (2, 1, 3):
            b_copies[u, d] = send(
                back_out.at[u, row_peer(d)],
                carry.at[u, r],
                b_send.at[u, d],
                b_recv.at[u, d],
                to_row(d),
            )
    for copy in b_copies.values():
        copy.wait_recv()
    for copy in sent:
        copy.wait_send()


def final_kernel(carry, mix, gate, outward, decays, gain, w_out, result, gated, normed):
    inner = mix.shape[2]
    heads = inner // STRETCH
    events = mix.shape[1]

    @pl.loop(0, events // STRETCH)
    def _(c):
        rows = pl.ds(pl.multiple_of(c * STRETCH, STRETCH), STRETCH)
        outs = outward[0, rows, :]
        squares = jnp.zeros((STRETCH, STRETCH), F32)
        for r in range(ROWS):
            carried = dot(outs, carry[0, r])
            for half in range(2):
                h = 2 * r + half
                cols = slice(h * STRETCH, (h + 1) * STRETCH)
                value = mix[0, rows, cols].astype(F32) + decays[0, rows, h : h + 1] * carried[
                    :, half * STRETCH : (half + 1) * STRETCH
                ]
                value = value * gate[0, rows, cols].astype(F32)
                squares = squares + value * value
                gated[:, cols] = value
        mean = jnp.sum(squares, axis=1, keepdims=True) * (1.0 / inner)
        scale = lax.rsqrt(mean + 1.0)
        for h in range(heads):
            cols = slice(h * STRETCH, (h + 1) * STRETCH)
            normed[rows, cols] = (gated[:, cols] * scale * gain[:, cols]).astype(BF16)

    usable = decays[0, :, heads : heads + 1]

    @pl.loop(0, w_out.shape[1] // CHUNK)
    def _(j):
        columns = pl.ds(pl.multiple_of(j * CHUNK, CHUNK), CHUNK)
        result[0, 0, :, columns] = (dot(normed[...], w_out[:, columns]) * usable).astype(BF16)


def per_device(
    item_ids,
    pad_masks,
    lengths,
    item_table,
    w_gate,
    w_in,
    w_dt,
    conv_taps,
    dt_bias,
    decay_rates,
    norm_gain,
    w_out,
):
    users, _, events = item_ids.shape
    inner = w_gate.shape[1]
    heads = decay_rates.shape[0]
    pair = 2 * STRETCH
    cols = lax.axis_size("col")
    route = [(r * cols + c, (r + 1) * cols + c) for r in range(ROWS - 1) for c in range(cols)]
    route += [((ROWS - 1) * cols + c, c + 1) for c in range(cols - 1)]
    ids_behind = lax.ppermute(
        item_ids[:, :, events - STRETCH :] + 1, ("row", "col"), route
    )
    vmem = pl.BlockSpec(memory_space=pltpu.VMEM)
    states, logs, mix, gate, outward, decays = pl.pallas_call(
        local_kernel,
        name="local",
        out_shape=(
            jax.ShapeDtypeStruct((ROWS, users, STRETCH, pair), BF16),
            jax.ShapeDtypeStruct((ROWS, users, 1, pair), F32),
            jax.ShapeDtypeStruct((users, events, inner), BF16),
            jax.ShapeDtypeStruct((users, events, inner), BF16),
            jax.ShapeDtypeStruct((users, events, STRETCH), BF16),
            jax.ShapeDtypeStruct((users, events, STRETCH), F32),
        ),
        in_specs=[pl.BlockSpec(memory_space=pltpu.SMEM)] + [vmem] * 10,
        out_specs=(vmem,) * 6,
        scratch_shapes=[
            pltpu.VMEM((inner, STRETCH), BF16),
            pltpu.VMEM((1, STRETCH), F32),
            pltpu.VMEM((1, STRETCH), F32),
            pltpu.VMEM((users, HALO + events, item_table.shape[0]), BF16),
            pltpu.VMEM((users, HALO + events, CHUNK), F32),
            pltpu.VMEM((users, events, inner), BF16),
            pltpu.VMEM((users, events, STRETCH), BF16),
            pltpu.VMEM((users, events, STRETCH), F32),
            pltpu.VMEM((STRETCH, inner), F32),
            pltpu.VMEM((1, STRETCH), F32),
        ],
    )(
        lengths,
        item_ids,
        ids_behind,
        pad_masks,
        item_table,
        w_gate,
        w_in,
        w_dt,
        conv_taps,
        dt_bias.reshape(1, heads),
        decay_rates.reshape(1, heads),
    )
    part = STRETCH // ZS
    dma = pltpu.SemaphoreType.DMA
    carry = pl.pallas_call(
        scan_kernel,
        name="scan",
        out_shape=jax.ShapeDtypeStruct((users, ROWS, STRETCH, pair), BF16),
        in_specs=[vmem] * 2,
        out_specs=vmem,
        scratch_shapes=[
            pltpu.VMEM((users, ROWS, STRETCH, pair), BF16),
            pltpu.VMEM((ROWS, users, 1, pair), F32),
            pltpu.VMEM((users, ROWS - 1, STRETCH, pair), F32),
            pltpu.VMEM((users, ZS, part, pair), BF16),
            pltpu.VMEM((users, ZS, part, pair), BF16),
            pltpu.VMEM((users, 1, pair), F32),
            pltpu.VMEM((ZS, users, 1, pair), F32),
            pltpu.VMEM((users, part, pair), BF16),
            pltpu.VMEM((users, YS, part, pair), BF16),
            pltpu.VMEM((users, 1, pair), F32),
            pltpu.VMEM((YS, users, 1, pair), F32),
            pltpu.VMEM((users, ZS, part, pair), BF16),
            pltpu.VMEM((users, ZS, part, pair), BF16),
            pltpu.VMEM((users, ROWS, STRETCH, pair), BF16),
            dma((users, ROWS)),
            dma((users, ROWS)),
            dma((ROWS,)),
            dma((ROWS,)),
            dma((users, ZS)),
            dma((users, ZS)),
            dma((ZS,)),
            dma((ZS,)),
            dma((users, YS)),
            dma((users, YS)),
            dma((YS,)),
            dma((YS,)),
            dma((users, ZS)),
            dma((users, ZS)),
            dma((users, ROWS)),
            dma((users, ROWS)),
        ],
        compiler_params=pltpu.CompilerParams(collective_id=0, has_side_effects=True),
    )(states, logs)
    by_user = lambda *shape: pl.BlockSpec((1, *shape), lambda u: (u,) + (0,) * len(shape))
    return pl.pallas_call(
        final_kernel,
        name="final",
        grid=(users,),
        out_shape=jax.ShapeDtypeStruct((users, 1, events, w_out.shape[1]), BF16),
        in_specs=[
            by_user(ROWS, STRETCH, pair),
            by_user(events, inner),
            by_user(events, inner),
            by_user(events, STRETCH),
            by_user(events, STRETCH),
            pl.BlockSpec((1, inner), lambda u: (0, 0)),
            pl.BlockSpec(w_out.shape, lambda u: (0, 0)),
        ],
        out_specs=by_user(1, events, w_out.shape[1]),
        scratch_shapes=[pltpu.VMEM((STRETCH, inner), F32), pltpu.VMEM((events, inner), BF16)],
    )(carry, mix, gate, outward, decays, norm_gain.reshape(1, inner), w_out)


def solution(mesh):
    spans = P("batch", "col", "row")
    return jax.shard_map(
        per_device,
        mesh=mesh,
        in_specs=(spans, spans, P("batch")) + (P(),) * 9,
        out_specs=P("batch", "col", "row", None),
        check_vma=False,
    )
```

time: 214 us -> 80.1 us (0.37)
  Pallas kernels: 0 us -> 67.2 us
  waiting for transfers between devices: 65.8 us -> 6.43 us
  local copies, waits for them, and re-layouts: 37.4 us -> 2.14 us
  blocking collectives: 33.4 us -> 0 us
  other arithmetic: 27.8 us -> 0.68 us
  matrix products: 25.3 us -> 0 us
  between operations: 13.6 us -> 0.02 us
  starting transfers between devices: 9.73 us -> 3.39 us
    pallas_call x0 -> x3, Pallas kernels: none -> 67.2 us  [the longest x1 31.7 us: per_device(): pl.pallas_call(scan_kernel, name='scan', out_shape=jax.ShapeDtypeStruct((...]
    all_gather x3 -> x0, waiting for transfers between devices: 51.2 us -> none  [the longest x2 26.7 us: carried_in(): pieces = jax.tree.map(lambda part: lax.all_gather(part, axis), subtotal)]
    all_gather x3 -> x0, blocking collectives: 33.4 us -> none  [the longest x2 24.7 us: carried_in(): pieces = jax.tree.map(lambda part: lax.all_gather(part, axis), subtotal)]
    dot_general x8 -> x0, matrix products: 25.3 us -> none  [the longest x1 4.68 us: per_device(): jnp.dot(embedded, w_gate, preferred_element_type=jnp.float32)]
    another operation x4 -> x0, other arithmetic: 11 us -> none
    unnamed x41 -> x3, local copies, waits for them, and re-layouts: 11.6 us -> 2.14 us
    all_to_all x1 -> x0, waiting for transfers between devices: 9.05 us -> none  [copy_for_each(): return lax.all_to_all(copies, axis, split_axis=0, concat_axis=0, tiled=True)]
    convert_element_type x6 -> x0, other arithmetic: 8.73 us -> none  [the longest x1 4.14 us: per_device(): normed = (gated_rows * lax.rsqrt(jnp.mean(gated_rows * gated_rows, axis=-...]
  transfers between devices with their start and end apart: 6 -> 1, of which waited for: 5 -> 1; matrix products, arithmetic and copies ran while one was open for 11% -> 2% of each run, Pallas kernels for 0% -> 0%
where the time goes in v1:
time: 80.1 us; the launch traced here: 79.9 us
  Pallas kernels  67.2 us (84%)
  waiting for transfers between devices  6.43 us (8%)
  starting transfers between devices  3.39 us (4%)
  local copies, waits for them, and re-layouts  2.14 us (3%)
    pallas_call x1, Pallas kernels, per_device(): pl.pallas_call(scan_kernel, name='scan', out_shape=jax.ShapeDtypeStruct((...  31.7 us
    pallas_call x1, Pallas kernels, per_device(): pl.pallas_call(local_kernel, name='local', out_shape=(jax.ShapeDtypeStruc...  24.9 us
    pallas_call x1, Pallas kernels, per_device(): pl.pallas_call(final_kernel, name='final', grid=(users,), out_shape=jax.S...  10.6 us
    ppermute x1, waiting for transfers between devices, per_device(): lax.ppermute(item_ids[:, :, events - STRETCH:] + 1, ('row', 'col'), route)  6.43 us
    ppermute x1, starting transfers between devices, per_device(): lax.ppermute(item_ids[:, :, events - STRETCH:] + 1, ('row', 'col'), route)  3.39 us
    unnamed x3, local copies, waits for them, and re-layouts  2.14 us
  transfers between devices with their start and end apart: 1, of which 1 were waited for; matrix products, arithmetic and copies ran while one was open for 2% of the time, Pallas kernels for 0%

profile of v1, /device:TPU:8, one launch (start us, length us, event | category | flops | bytes accessed | tf_op | source)
XLA Modules:
  0.0 79.9 jit_solution(13851339637992706197)
XLA Ops:
  0.0 0.7 slice_add_fusion
  0.7 3.4 %collective-permute-start = (s32[2,1,128]{2,1,0:T(1,128)S(1)}, s32[2,1,128]{2,1,0:T(1,128)S(1)}, u32[]{:S(2)}, u32[]{:S(2)}) collective-permute-start(s32[2,1,128]{2,1,0:T(1,128)S(1)} %slice_add_fusion), channel_id=1, source_target_pairs={{0,64},{2,66},{4,68},{6,70},{8,72},{10,74},{12,76},{14,78},{16,80}... | collective-permute-start | bytes 3080 | tf_op jit(solution)/shard_map/ppermute | solution.py:466
  4.1 1.6 %copy.13.w_dt = bf16[1024,8]{1,0:T(8,128)(2,1)} copy(bf16[1024,8]{0,1:T(8,128)(2,1)} %param.18) | data formatting | bytes 32768 | tf_op args[6]
  5.6 6.4 %collective-permute-done.halo = s32[2,1,128]{2,1,0:T(1,128)S(1)} collective-permute-done((s32[2,1,128]{2,1,0:T(1,128)S(1)}, s32[2,1,128]{2,1,0:T(1,128)S(1)}, u32[]{:S(2)}, u32[]{:S(2)}) %collective-permute-start) | collective-permute-done | bytes 1056 | tf_op jit(solution)/shard_map/ppermute | solution.py:466
  12.1 0.0 copy-start
  12.1 0.6 copy-done
  12.7 24.9 %local.1 = (bf16[4,2,128,256]{3,2,1,0:T(8,128)(2,1)}, f32[4,2,1,256]{3,2,1,0:T(1,128)}, bf16[2,512,1024]{2,1,0:T(8,128)(2,1)}, bf16[2,512,1024]{2,1,0:T(8,128)(2...) custom-call(s32[2]{0:T(128)} %lengths.1, s32[2,1,512]{2,1,0:T(1,128)} %ids.1, s32[2,1,128]{2,1,0:T(1,128)} %copy-done, ...), custom_call_target="tpu_custom_call" | custom-call | tf_op jit(solution)/shard_map/local/pallas_call | solution.py:470
  37.6 31.7 %scan.1.carry = bf16[2,4,128,256]{3,2,1,0:T(8,128)(2,1)} custom-call(bf16[4,2,128,256]{3,2,1,0:T(8,128)(2,1)} %get-tuple-element.11.states, f32[4,2,1,256]{3,2,1,0:T(1,128)} %get-tuple-element.12.logs), custom_call_target="tpu_custom_call" | custom-call | tf_op jit(solution)/shard_map/scan/pallas_call | solution.py:510
  69.2 10.6 %final.1 = bf16[2,1,512,1024]{3,2,1,0:T(8,128)(2,1)} custom-call(bf16[2,4,128,256]{3,2,1,0:T(8,128)(2,1)} %scan.1.carry, bf16[2,512,1024]{2,1,0:T(8,128)(2,1)} %get-tuple-element.13.mix, bf16[2,512,1024]{2,1,0:T(8,128)(2,1)} %get-tuple-element.14.gate, bf16[2,512,128]{2,1,0:T(8,128)(2,1)} %get-tuple-element.15.outward, ...), custom_call_target="tpu_custom_call" | custom-call | tf_op jit(solution)/shard_map/final/pallas_call | solution.py:551
Async XLA Ops:
  0.7 11.4 %collective-permute-start = (s32[2,1,128]{2,1,0:T(1,128)S(1)}, s32[2,1,128]{2,1,0:T(1,128)S(1)}, u32[]{:S(2)}, u32[]{:S(2)}) collective-permute-start(s32[2,1,128]{2,1,0:T(1,128)S(1)} %slice_add_fusion), channel_id=1, source_target_pairs={{0,64},{2,66},{4,68},{6,70},{8,72},{10,74},{12,76},{14,78},{16,80}... | collective-permute-start | bytes 3080 | tf_op jit(solution)/shard_map/ppermute | solution.py:466
  12.1 0.6 copy-start

commit v2 on v1

v2 whole, which is shorter than its diff:
```python
import jax
import jax.numpy as jnp
from jax import lax
from jax.experimental import pallas as pl
from jax.experimental.pallas import tpu as pltpu
from jax.sharding import PartitionSpec as P

STRETCH = 128
CHUNK = 256
HALO = 16
ROWS, YS, ZS = 4, 4, 8
MESH = pl.DeviceIdType.MESH
BF16 = jnp.bfloat16
F32 = jnp.float32


def silu(v):
    return v * (0.5 * jnp.tanh(0.5 * v) + 0.5)


def dot(a, b):
    return jnp.dot(a, b, preferred_element_type=F32)


def down_columns(row):
    return jnp.transpose(jnp.broadcast_to(row, (STRETCH, STRETCH)))


def main_kernel(
    lengths,
    ids,
    pads,
    w_dt,
    taps,
    bias,
    rates,
    table_in,
    w_in_in,
    w_gate_in,
    carry,
    mix,
    gate,
    outward,
    decays,
    table,
    w_in,
    w_gate,
    wdt_wide,
    bias_wide,
    rates_wide,
    split_steps,
    halo,
    hot,
    projected,
    joined_even,
    joined_odd,
    signal,
    inward,
    steps,
    log_columns,
    log_rows,
    step_rows,
    inside,
    running,
    passed,
    states,
    logs,
    row_states,
    row_logs,
    row_before,
    z_out,
    z_states,
    z_before,
    z_log_out,
    z_logs,
    y_out,
    y_states,
    y_log_out,
    y_logs,
    c_out,
    c_states,
    back_out,
    load_sem,
    halo_send,
    halo_recv,
    x_send,
    x_recv,
    xl_send,
    xl_recv,
    z_send,
    z_recv,
    zl_send,
    zl_recv,
    y_send,
    y_recv,
    yl_send,
    yl_recv,
    c_send,
    c_recv,
    b_send,
    b_recv,
):
    users, _, events = ids.shape
    inner = w_gate.shape[1]
    heads = w_dt.shape[0]
    stretches = events // STRETCH
    chunks = w_in.shape[1] // CHUNK
    part = z_states.shape[2]
    r = lax.axis_index("row")
    col = lax.axis_index("col")
    cols_axis = lax.axis_size("col")
    y, z = col // ZS, lax.rem(col, ZS)
    first = (col * ROWS + r) * events

    loads = [pltpu.make_async_copy(table_in, table, load_sem.at[0])]
    for j in range(chunks):
        columns = slice(j * CHUNK, (j + 1) * CHUNK)
        loads.append(
            pltpu.make_async_copy(w_in_in.at[:, columns], w_in.at[:, columns], load_sem.at[1 + j])
        )
    loads.append(pltpu.make_async_copy(w_gate_in, w_gate, load_sem.at[1 + chunks]))
    for load in loads:
        load.start()

    def row_peer(d):
        return lax.rem(r + d, ROWS)

    def z_peer(d):
        return lax.rem(z + d, ZS)

    def to_row(d):
        return {"row": row_peer(d)}

    def to_z(d):
        return {"col": y * ZS + z_peer(d)}

    def to_y(d):
        return {"col": lax.rem(y + d, YS) * ZS + z}

    next_span = {
        "row": row_peer(1),
        "col": lax.rem(col + jnp.where(r == ROWS - 1, 1, 0), cols_axis),
    }
    last_span = {
        "row": row_peer(ROWS - 1),
        "col": lax.rem(col + jnp.where(r == 0, cols_axis - 1, 0), cols_axis),
    }
    barrier = pltpu.get_barrier_semaphore()
    peers = (
        [to_row(d) for d in range(1, ROWS)]
        + [to_z(d) for d in range(1, ZS)]
        + [to_y(d) for d in range(1, YS)]
        + [next_span, last_span]
    )
    for peer in peers:
        pl.semaphore_signal(barrier, inc=1, device_id=peer, device_id_type=MESH)

    sent = []

    def send(src, dst, send_sem, recv_sem, device):
        copy = pltpu.make_async_remote_copy(
            src_ref=src,
            dst_ref=dst,
            send_sem=send_sem,
            recv_sem=recv_sem,
            device_id=device,
            device_id_type=MESH,
        )
        copy.start()
        sent.append(copy)
        return copy

    lanes = lax.broadcasted_iota(jnp.int32, (STRETCH, STRETCH), 1)
    lanes_f = lanes.astype(F32)
    causal = lax.broadcasted_iota(jnp.int32, (STRETCH, STRETCH), 0) >= lanes

    def one_hot(row, u, begin, rows):
        column = down_columns(row)[STRETCH - rows :, :]
        for j in range(table.shape[0] // STRETCH):
            match = column == lanes_f[:rows] + float(j * STRETCH)
            hot[u, begin : begin + rows, j * STRETCH : (j + 1) * STRETCH] = jnp.where(
                match, 1.0, 0.0
            ).astype(BF16)

    for u in range(users):
        for c in range(stretches):
            row = ids[u, :, c * STRETCH : (c + 1) * STRETCH].astype(F32)
            one_hot(row, u, HALO + c * STRETCH, STRETCH)
    wdt_wide[...] = jnp.zeros_like(wdt_wide)
    wdt_wide[0:heads, :] = w_dt[...]
    bias_wide[...] = jnp.zeros_like(bias_wide)
    bias_wide[:, 0:heads] = bias[...]
    rates_wide[...] = jnp.zeros_like(rates_wide)
    rates_wide[:, 0:heads] = rates[...]

    pl.semaphore_wait(barrier, len(peers))
    tail = slice(events - STRETCH, events)
    halo_copy = send(ids.at[:, :, tail], halo, halo_send, halo_recv, next_span)

    loads[0].wait()
    raw = lax.dot_general(
        table[...], wdt_wide[...], (((1,), (1,)), ((), ())), preferred_element_type=F32
    )
    raw = raw + bias_wide[...]
    soft = jnp.maximum(raw, 0.0) + jnp.log1p(jnp.exp(-jnp.abs(raw)))
    high = soft.astype(BF16)
    rest = soft - high.astype(F32)
    middle = rest.astype(BF16)
    split_steps[:, 0:STRETCH] = high
    split_steps[:, STRETCH : 2 * STRETCH] = middle
    split_steps[:, 2 * STRETCH :] = (rest - middle.astype(F32)).astype(BF16)
    for u in range(users):
        picked = dot(hot[u, HALO:, :], split_steps[...])
        step = picked[:, 0:STRETCH] + (
            picked[:, STRETCH : 2 * STRETCH] + picked[:, 2 * STRETCH :]
        )
        for c in range(stretches):
            place = first + c * STRETCH + lax.broadcasted_iota(jnp.int32, (1, STRETCH), 1)
            rows = slice(c * STRETCH, (c + 1) * STRETCH)
            kept = jnp.logical_and(place < lengths[u], pads[u, :, rows] > 0)
            usable = down_columns(jnp.where(kept, 1.0, 0.0))
            steps[u, rows, :] = jnp.where(
                lanes == heads, usable, jnp.where(lanes < heads, step[rows] * usable, 0.0)
            )

    for j in range(chunks):
        columns = slice(j * CHUNK, (j + 1) * CHUNK)
        loads[1 + j].wait()
        projected[:, columns] = dot(table[...], w_in[:, columns]).astype(BF16)

    halo_copy.wait_recv()
    nobody = jnp.logical_and(r == 0, col == 0)
    for u in range(users):
        one_hot(jnp.where(nobody, -1.0, halo[u].astype(F32)), u, 0, HALO)

    joined = (joined_even, joined_odd)

    def gather(u, j):
        joined[j % 2][...] = dot(hot[u], projected[:, j * CHUNK : (j + 1) * CHUNK])

    def convolve(u, j):
        columns = slice(j * CHUNK, (j + 1) * CHUNK)
        total = None
        for k in range(taps.shape[0]):
            begin = HALO - taps.shape[0] + 1 + k
            term = joined[j % 2][begin : begin + events, :] * taps[k : k + 1, columns]
            total = term if total is None else total + term
        if j < chunks - 1:
            signal[u, :, columns] = silu(total).astype(BF16)
        else:
            maps = total.astype(BF16)
            inward[u] = maps[:, 0:STRETCH]
            outward[u] = maps[:, STRETCH:]

    def state_phase(u):
        gather(u, 0)
        for j in range(chunks):
            if j + 1 < chunks:
                gather(u, j + 1)
            convolve(u, j)
        lower = jnp.where(causal, 1.0, 0.0)
        passed[...] = jnp.zeros_like(passed)

        @pl.loop(0, stretches)
        def _(c):
            rows = pl.ds(pl.multiple_of(c * STRETCH, STRETCH), STRETCH)
            step = steps[u, rows, :]
            log = jnp.dot(
                lower,
                step * rates_wide[...],
                preferred_element_type=F32,
                precision=lax.Precision.HIGHEST,
            )
            before = passed[...]
            decays[u, rows, :] = jnp.where(lanes == heads, step, jnp.exp(-(log + before)))
            passed[...] = before + log[STRETCH - 1 :, :]
            log_columns[u, rows, :] = log
            log_t = jnp.transpose(log)[0:heads]
            step_t = jnp.transpose(step)[0:heads]
            log_rows[u, c] = log_t
            step_rows[u, c] = step_t
            last = log_t[:, STRETCH - 1 :]
            tail_t = jnp.exp(log_t - last) * step_t
            stay = jnp.exp(-last)
            in_t = jnp.transpose(inward[u, rows, :].astype(F32))
            for h in range(heads):
                cols = slice(h * STRETCH, (h + 1) * STRETCH)
                entering = jnp.where(c == 0, 0.0, running[:, cols])
                inside[u, c, :, cols] = entering.astype(BF16)
                scaled = (in_t * tail_t[h : h + 1, :]).astype(BF16)
                running[:, cols] = stay[h : h + 1, :] * entering + dot(
                    scaled, signal[u, rows, cols]
                )

        for h in range(heads):
            half = h % 2
            cols = slice(half * STRETCH, (half + 1) * STRETCH)
            states[h // 2, u, :, cols] = running[:, h * STRETCH : (h + 1) * STRETCH].astype(BF16)
            logs[h // 2, u, :, cols] = jnp.broadcast_to(passed[:, h : h + 1], (1, STRETCH))

    def local_phase(u, begin, end):
        @pl.loop(begin, end)
        def _(c):
            rows = pl.ds(pl.multiple_of(c * STRETCH, STRETCH), STRETCH)
            log = log_columns[u, rows, :]
            fade = jnp.exp(-log)
            log_t = log_rows[u, c]
            step_t = step_rows[u, c]
            outs = outward[u, rows, :]
            scores = lax.dot_general(
                outs, inward[u, rows, :], (((1,), (1,)), ((), ())), preferred_element_type=F32
            )
            for h in range(heads):
                cols = slice(h * STRETCH, (h + 1) * STRETCH)
                gap = jnp.where(causal, log_t[h : h + 1, :] - log[:, h : h + 1], -1e30)
                weights = (scores * jnp.exp(gap) * step_t[h : h + 1, :]).astype(BF16)
                mix[u, rows, cols] = (
                    dot(weights, signal[u, rows, cols])
                    + dot(outs, inside[u, c, :, cols]) * fade[:, h : h + 1]
                ).astype(BF16)

    x_copies, xl_copies, z_copies, y_copies, c_copies, b_copies = {}, {}, {}, {}, {}, {}
    for u in range(users):
        state_phase(u)
        for d in (2, 1, 3):
            xl_copies[u, d] = send(
                logs.at[row_peer(d), u],
                row_logs.at[u, r],
                xl_send.at[u, d],
                xl_recv.at[u, d],
                to_row(d),
            )
            x_copies[u, d] = send(
                states.at[row_peer(d), u],
                row_states.at[u, r],
                x_send.at[u, d],
                x_recv.at[u, d],
                to_row(d),
            )
        row_logs[u, r] = logs[r, u]
        row_states[u, r] = states[r, u]

    def row_step(u):
        for d in range(1, ROWS):
            xl_copies[u, d].wait_recv()
            x_copies[u, d].wait_recv()
        block_log = row_logs[u, 0]
        for i in range(1, ROWS):
            block_log = block_log + row_logs[u, i]
        z_log_out[u] = block_log
        z_logs[u, z] = block_log
        total = row_states[u, 0].astype(F32)
        for i in range(1, ROWS):
            row_before[u, i - 1] = total
            total = jnp.exp(-row_logs[u, i]) * total + row_states[u, i].astype(F32)
        block = total.astype(BF16)
        for k in range(ZS):
            z_out[u, k] = block[k * part : (k + 1) * part]
        z_states[u, z] = z_out[u, z]
        for d in (4, 3, 5, 2, 6, 1, 7):
            z_copies[u, d] = (
                send(
                    z_log_out.at[u], z_logs.at[u, z], zl_send.at[u, d], zl_recv.at[u, d], to_z(d)
                ),
                send(
                    z_out.at[u, z_peer(d)],
                    z_states.at[u, z],
                    z_send.at[u, d],
                    z_recv.at[u, d],
                    to_z(d),
                ),
            )

    def z_step(u):
        for d in range(1, ZS):
            for copy in z_copies[u, d]:
                copy.wait_recv()
        y_log = z_logs[u, 0]
        for i in range(1, ZS):
            y_log = y_log + z_logs[u, i]
        y_log_out[u] = y_log
        y_logs[u, y] = y_log
        total = z_states[u, 0].astype(F32)
        for i in range(1, ZS):
            z_before[u, i - 1] = total
            total = jnp.exp(-z_logs[u, i]) * total + z_states[u, i].astype(F32)
        y_out[u] = total.astype(BF16)
        for d in (2, 1, 3):
            y_copies[u, d] = (
                send(
                    y_log_out.at[u], y_logs.at[u, y], yl_send.at[u, d], yl_recv.at[u, d], to_y(d)
                ),
                send(y_out.at[u], y_states.at[u, y], y_send.at[u, d], y_recv.at[u, d], to_y(d)),
            )

    def y_step(u):
        for d in range(1, YS):
            for copy in y_copies[u, d]:
                copy.wait_recv()
        entering = jnp.zeros(y_out.shape[1:], F32)
        for i in range(YS - 1):
            entering = jnp.where(
                i < y, jnp.exp(-y_logs[u, i]) * entering + y_states[u, i].astype(F32), entering
            )
        gone = None
        for k in range(ZS):
            value = entering
            if k:
                gone = z_logs[u, k - 1] if gone is None else gone + z_logs[u, k - 1]
                value = jnp.exp(-gone) * entering + z_before[u, k - 1]
            c_out[u, k] = value.astype(BF16)
        c_states[u, z] = c_out[u, z]
        for d in (4, 3, 5, 2, 6, 1, 7):
            c_copies[u, d] = send(
                c_out.at[u, z_peer(d)],
                c_states.at[u, z],
                c_send.at[u, d],
                c_recv.at[u, d],
                to_z(d),
            )

    def back_step(u):
        for d in range(1, ZS):
            c_copies[u, d].wait_recv()
        gone = None
        for i in range(ROWS):
            if i:
                gone = row_logs[u, i - 1] if gone is None else gone + row_logs[u, i - 1]
            for k in range(ZS):
                rows = slice(k * part, (k + 1) * part)
                value = c_states[u, k].astype(F32)
                if i:
                    value = jnp.exp(-gone) * value + row_before[u, i - 1, rows, :]
                back_out[u, i, rows, :] = value.astype(BF16)
        carry[u, r] = back_out[u, r]
        for d in (2, 1, 3):
            b_copies[u, d] = send(
                back_out.at[u, row_peer(d)],
                carry.at[u, r],
                b_send.at[u, d],
                b_recv.at[u, d],
                to_row(d),
            )

    loads[-1].wait()

    @pl.loop(0, inner // CHUNK)
    def _(j):
        columns = pl.ds(pl.multiple_of(j * CHUNK, CHUNK), CHUNK)
        opened = dot(table[...], w_gate[:, columns]).astype(BF16)
        opened = silu(opened.astype(F32)).astype(BF16)
        for u in range(users):
            gate[u, :, columns] = dot(hot[u, HALO:, :], opened).astype(BF16)

    half = stretches // 2
    row_step(0)
    local_phase(0, 0, half)
    row_step(1)
    local_phase(0, half, stretches)
    z_step(0)
    z_step(1)
    local_phase(1, 0, half)
    y_step(0)
    y_step(1)
    local_phase(1, half, stretches)
    back_step(0)
    back_step(1)
    for copy in b_copies.values():
        copy.wait_recv()
    for copy in sent:
        copy.wait_send()


def final_kernel(carry, mix, gate, outward, decays, gain, w_out, result, gated, normed, done, sems):
    users, events, inner = mix.shape
    heads = inner // STRETCH
    width = w_out.shape[1]

    def norm(u, c):
        rows = slice(c * STRETCH, (c + 1) * STRETCH)
        outs = outward[u, rows, :]
        squares = jnp.zeros((STRETCH, STRETCH), F32)
        for r in range(ROWS):
            carried = dot(outs, carry[u, r])
            for half in range(2):
                h = 2 * r + half
                cols = slice(h * STRETCH, (h + 1) * STRETCH)
                value = mix[u, rows, cols].astype(F32) + decays[u, rows, h : h + 1] * carried[
                    :, half * STRETCH : (half + 1) * STRETCH
                ]
                value = value * gate[u, rows, cols].astype(F32)
                squares = squares + value * value
                gated[c % 2, :, cols] = value
        mean = jnp.sum(squares, axis=1, keepdims=True) * (1.0 / inner)
        scale = lax.rsqrt(mean + 1.0)
        for h in range(heads):
            cols = slice(h * STRETCH, (h + 1) * STRETCH)
            normed[u, rows, cols] = (gated[c % 2, :, cols] * scale * gain[:, cols]).astype(BF16)

    copies = []

    def project(u, j):
        columns = slice(j * CHUNK, (j + 1) * CHUNK)
        usable = decays[u, :, heads : heads + 1]
        done[u, :, columns] = (dot(normed[u], w_out[:, columns]) * usable).astype(BF16)
        return columns

    def store(u, j, columns):
        copy = pltpu.make_async_copy(
            done.at[u, :, columns], result.at[u, 0, :, columns], sems.at[u, j]
        )
        copy.start()
        copies.append(copy)

    blocks = events // STRETCH
    for c in range(blocks):
        norm(0, c)
    for u in range(users):
        for j in range(width // CHUNK):
            columns = project(u, j)
            if u + 1 < users and j < blocks:
                norm(u + 1, j)
            store(u, j, columns)
    for copy in copies:
        copy.wait()


def per_device(
    item_ids,
    pad_masks,
    lengths,
    item_table,
    w_gate,
    w_in,
    w_dt,
    conv_taps,
    dt_bias,
    decay_rates,
    norm_gain,
    w_out,
):
    users, _, events = item_ids.shape
    items, width = item_table.shape
    inner = w_gate.shape[1]
    full = w_in.shape[1]
    heads = decay_rates.shape[0]
    stretches = events // STRETCH
    pair = 2 * STRETCH
    part = STRETCH // ZS
    vmem = pl.BlockSpec(memory_space=pltpu.VMEM)
    hbm = pl.BlockSpec(memory_space=pltpu.HBM)
    dma = pltpu.SemaphoreType.DMA
    carry, mix, gate, outward, decays = pl.pallas_call(
        main_kernel,
        name="main",
        out_shape=(
            jax.ShapeDtypeStruct((users, ROWS, STRETCH, pair), BF16),
            jax.ShapeDtypeStruct((users, events, inner), BF16),
            jax.ShapeDtypeStruct((users, events, inner), BF16),
            jax.ShapeDtypeStruct((users, events, STRETCH), BF16),
            jax.ShapeDtypeStruct((users, events, STRETCH), F32),
        ),
        in_specs=[pl.BlockSpec(memory_space=pltpu.SMEM)] + [vmem] * 6 + [hbm] * 3,
        out_specs=(vmem,) * 5,
        scratch_shapes=[
            pltpu.VMEM((items, width), BF16),
            pltpu.VMEM((width, full), BF16),
            pltpu.VMEM((width, inner), BF16),
            pltpu.VMEM((STRETCH, width), BF16),
            pltpu.VMEM((1, STRETCH), F32),
            pltpu.VMEM((1, STRETCH), F32),
            pltpu.VMEM((items, 3 * STRETCH), BF16),
            pltpu.VMEM((users, 1, STRETCH), jnp.int32),
            pltpu.VMEM((users, HALO + events, items), BF16),
            pltpu.VMEM((items, full), BF16),
            pltpu.VMEM((HALO + events, CHUNK), F32),
            pltpu.VMEM((HALO + events, CHUNK), F32),
            pltpu.VMEM((users, events, inner), BF16),
            pltpu.VMEM((users, events, STRETCH), BF16),
            pltpu.VMEM((users, events, STRETCH), F32),
            pltpu.VMEM((users, events, STRETCH), F32),
            pltpu.VMEM((users, stretches, heads, STRETCH), F32),
            pltpu.VMEM((users, stretches, heads, STRETCH), F32),
            pltpu.VMEM((users, stretches, STRETCH, inner), BF16),
            pltpu.VMEM((STRETCH, inner), F32),
            pltpu.VMEM((1, STRETCH), F32),
            pltpu.VMEM((ROWS, users, STRETCH, pair), BF16),
            pltpu.VMEM((ROWS, users, 1, pair), F32),
            pltpu.VMEM((users, ROWS, STRETCH, pair), BF16),
            pltpu.VMEM((users, ROWS, 1, pair), F32),
            pltpu.VMEM((users, ROWS - 1, STRETCH, pair), F32),
            pltpu.VMEM((users, ZS, part, pair), BF16),
            pltpu.VMEM((users, ZS, part, pair), BF16),
            pltpu.VMEM((users, ZS - 1, part, pair), F32),
            pltpu.VMEM((users, 1, pair), F32),
            pltpu.VMEM((users, ZS, 1, pair), F32),
            pltpu.VMEM((users, part, pair), BF16),
            pltpu.VMEM((users, YS, part, pair), BF16),
            pltpu.VMEM((users, 1, pair), F32),
            pltpu.VMEM((users, YS, 1, pair), F32),
            pltpu.VMEM((users, ZS, part, pair), BF16),
            pltpu.VMEM((users, ZS, part, pair), BF16),
            pltpu.VMEM((users, ROWS, STRETCH, pair), BF16),
            dma((2 + full // CHUNK,)),
            dma,
            dma,
        ]
        + [dma((users, ROWS))] * 4
        + [dma((users, ZS))] * 4
        + [dma((users, YS))] * 4
        + [dma((users, ZS))] * 2
        + [dma((users, ROWS))] * 2,
        compiler_params=pltpu.CompilerParams(
            collective_id=0, has_side_effects=True, vmem_limit_bytes=36 << 20
        ),
    )(
        lengths,
        item_ids,
        pad_masks,
        w_dt.T,
        conv_taps,
        dt_bias.reshape(1, heads),
        decay_rates.reshape(1, heads),
        item_table,
        w_in,
        w_gate,
    )
    return pl.pallas_call(
        final_kernel,
        name="final",
        out_shape=jax.ShapeDtypeStruct((users, 1, events, w_out.shape[1]), BF16),
        in_specs=[vmem] * 7,
        out_specs=hbm,
        scratch_shapes=[
            pltpu.VMEM((2, STRETCH, inner), F32),
            pltpu.VMEM((users, events, inner), BF16),
            pltpu.VMEM((users, events, w_out.shape[1]), BF16),
            dma((users, w_out.shape[1] // CHUNK)),
        ],
        compiler_params=pltpu.CompilerParams(vmem_limit_bytes=24 << 20),
    )(carry, mix, gate, outward, decays, norm_gain.reshape(1, inner), w_out)


def solution(mesh):
    spans = P("batch", "col", "row")
    return jax.shard_map(
        per_device,
        mesh=mesh,
        in_specs=(spans, spans, P("batch")) + (P(),) * 9,
        out_specs=P("batch", "col", "row", None),
        check_vma=False,
    )
```

time: 80.1 us -> 67.6 us (0.84)
  Pallas kernels: 67.2 us -> 57.6 us
  local copies, waits for them, and re-layouts: 2.14 us -> 9.34 us
  waiting for transfers between devices: 6.43 us -> 0 us
  starting transfers between devices: 3.39 us -> 0 us
    pallas_call x3 -> x2, Pallas kernels: 67.2 us -> 57.6 us  [the longest x1 52 us: per_device(): pl.pallas_call(main_kernel, name='main', out_shape=(jax.ShapeDtypeStruct(...]
    unnamed x3 -> x24, local copies, waits for them, and re-layouts: 2.14 us -> 9.34 us
    ppermute x1 -> x0, waiting for transfers between devices: 6.43 us -> none  [per_device(): lax.ppermute(item_ids[:, :, events - STRETCH:] + 1, ('row', 'col'), route)]
    ppermute x1 -> x0, starting transfers between devices: 3.39 us -> none  [per_device(): lax.ppermute(item_ids[:, :, events - STRETCH:] + 1, ('row', 'col'), route)]
  transfers between devices with their start and end apart: 1 -> 0, of which waited for: 1 -> 0; matrix products, arithmetic and copies ran while one was open for 2% -> 0% of each run, Pallas kernels for 0% -> 0%
where the time goes in v2:
time: 67.6 us; the launch traced here: 67.2 us
  Pallas kernels  57.6 us (85%)
  local copies, waits for them, and re-layouts  9.34 us (14%)
    pallas_call x1, Pallas kernels, per_device(): pl.pallas_call(main_kernel, name='main', out_shape=(jax.ShapeDtypeStruct(...  52 us
    unnamed x24, local copies, waits for them, and re-layouts  9.34 us
    pallas_call x1, Pallas kernels, per_device(): pl.pallas_call(final_kernel, name='final', out_shape=jax.ShapeDtypeStruct...  5.69 us

profile of v2, /device:TPU:8, one launch (start us, length us, event | category | flops | bytes accessed | tf_op | source)
XLA Modules:
  0.0 67.2 jit_solution(14436501486085014315)
XLA Ops:
  0.0 0.0 copy-start
  0.0 1.7 %copy-done = bf16[1024,1280]{1,0:T(8,128)(2,1)S(1)} copy-done((bf16[1024,1280]{1,0:T(8,128)(2,1)S(1)}, bf16[1024,1280]{1,0:T(8,128)(2,1)}, u32[]{:S(2)}) %copy-start) | copy-done | bytes 2621464
  1.7 0.0 copy-start.1
  1.7 1.6 %copy-done.1 = bf16[1024,1024]{1,0:T(8,128)(2,1)S(1)} copy-done((bf16[1024,1024]{1,0:T(8,128)(2,1)S(1)}, bf16[1024,1024]{1,0:T(8,128)(2,1)}, u32[]{:S(2)}) %copy-start.1) | copy-done | bytes 2097176
  3.3 0.0 copy-start.3
  3.3 1.2 %copy-done.3 = bf16[512,1024]{1,0:T(8,128)(2,1)S(1)} copy-done((bf16[512,1024]{1,0:T(8,128)(2,1)S(1)}, bf16[512,1024]{1,0:T(8,128)(2,1)}, u32[]{:S(2)}) %copy-start.3) | copy-done | bytes 1048600
  4.6 0.0 copy-start.4
  4.6 0.7 %copy-done.4 = f32[4,1280]{1,0:T(4,128)S(1)} copy-done((f32[4,1280]{1,0:T(4,128)S(1)}, f32[4,1280]{1,0:T(4,128)}, u32[]{:S(2)}) %copy-start.4) | copy-done | bytes 20504
  5.3 0.0 copy-start.5
  5.3 0.7 %copy-done.5 = bf16[1024,8]{0,1:T(8,128)(2,1)S(1)} copy-done((bf16[1024,8]{0,1:T(8,128)(2,1)S(1)}, bf16[1024,8]{0,1:T(8,128)(2,1)}, u32[]{:S(2)}) %copy-start.5) | copy-done | bytes 16408
  6.0 0.0 copy-start.7
  6.0 0.7 %copy-done.7 = s32[2,1,512]{2,1,0:T(1,128)S(1)} copy-done((s32[2,1,512]{2,1,0:T(1,128)S(1)}, s32[2,1,512]{2,1,0:T(1,128)}, u32[]{:S(2)}) %copy-start.7) | copy-done | bytes 4120
  6.7 0.0 copy-start.8
  6.7 0.7 %copy-done.8 = s32[2,1,512]{2,1,0:T(1,128)S(1)} copy-done((s32[2,1,512]{2,1,0:T(1,128)S(1)}, s32[2,1,512]{2,1,0:T(1,128)}, u32[]{:S(2)}) %copy-start.8) | copy-done | bytes 4120
  7.4 0.0 copy-start.9
  7.4 0.7 copy-done.9
  8.0 0.0 copy-start.10
  8.0 0.7 copy-done.10
  8.7 0.0 copy-start.11
  8.7 0.7 copy-done.11
  9.3 0.0 copy-start.2
  9.3 0.0 copy-start.6
  9.3 52.0 %main.1 = (bf16[2,4,128,256]{3,2,1,0:T(8,128)(2,1)S(1)}, bf16[2,512,1024]{2,1,0:T(8,128)(2,1)S(1)}, bf16[2,512,1024]{2,1,0:T(8,128)(2,1)S(1)}, bf16[2,512,128]{2,1,0:T(8,128)(2,1)S(1)}, f32[2,512,128]{2,1,0:T(8,128)S(1)}) custom-call(s32[2]{0:T(128)S(1)} %copy-done.9, s32[2,1,512]{2,1,0:T(1,128)S(1)} %copy-done.7, s32[2,1,512]{2,1,0:T(1,128)S(1)} %copy-done.8, ...), custom_call_target="tpu_custom_call" | custom-call | tf_op jit(solution)/shard_map/main/pallas_call | solution.py:553
  61.3 0.0 copy-done.2
  61.3 0.0 copy-done.6
  61.3 5.7 %final.1 = bf16[2,1,512,1024]{3,2,1,0:T(8,128)(2,1)} custom-call(bf16[2,4,128,256]{3,2,1,0:T(8,128)(2,1)S(1)} %get-tuple-element.10.carry, bf16[2,512,1024]{2,1,0:T(8,128)(2,1)S(1)} %get-tuple-element.11.mix, bf16[2,512,1024]{2,1,0:T(8,128)(2,1)S(1)} %get-tuple-element.12.gate, bf16[2,512,128]{2,1,0:T(8,128)(2,1)S(1)} %get-tuple-element.13.outward, ...), custom_call_target="tpu_custom_call" | custom-call | tf_op jit(solution)/shard_map/final/pallas_call | solution.py:628
Async XLA Ops:
  0.0 1.7 %copy-start = (bf16[1024,1280]{1,0:T(8,128)(2,1)S(1)}, bf16[1024,1280]{1,0:T(8,128)(2,1)}, u32[]{:S(2)}) copy-start(bf16[1024,1280]{1,0:T(8,128)(2,1)} %w_in_in.1) | copy-start | bytes 7864324
  1.7 1.6 %copy-start.1 = (bf16[1024,1024]{1,0:T(8,128)(2,1)S(1)}, bf16[1024,1024]{1,0:T(8,128)(2,1)}, u32[]{:S(2)}) copy-start(bf16[1024,1024]{1,0:T(8,128)(2,1)} %w_gate_in.1) | copy-start | bytes 6291460
  3.3 1.2 %copy-start.3 = (bf16[512,1024]{1,0:T(8,128)(2,1)S(1)}, bf16[512,1024]{1,0:T(8,128)(2,1)}, u32[]{:S(2)}) copy-start(bf16[512,1024]{1,0:T(8,128)(2,1)} %table_in.1) | copy-start | bytes 3145732
  4.6 0.7 %copy-start.4 = (f32[4,1280]{1,0:T(4,128)S(1)}, f32[4,1280]{1,0:T(4,128)}, u32[]{:S(2)}) copy-start(f32[4,1280]{1,0:T(4,128)} %taps.1) | copy-start | bytes 61444
  5.3 0.7 %copy-start.5 = (bf16[1024,8]{0,1:T(8,128)(2,1)S(1)}, bf16[1024,8]{0,1:T(8,128)(2,1)}, u32[]{:S(2)}) copy-start(bf16[1024,8]{0,1:T(8,128)(2,1)} %param.18) | copy-start | bytes 49156
  6.0 0.7 %copy-start.7 = (s32[2,1,512]{2,1,0:T(1,128)S(1)}, s32[2,1,512]{2,1,0:T(1,128)}, u32[]{:S(2)}) copy-start(s32[2,1,512]{2,1,0:T(1,128)} %ids.1) | copy-start | bytes 12292
  6.7 0.7 %copy-start.8 = (s32[2,1,512]{2,1,0:T(1,128)S(1)}, s32[2,1,512]{2,1,0:T(1,128)}, u32[]{:S(2)}) copy-start(s32[2,1,512]{2,1,0:T(1,128)} %pads.1) | copy-start | bytes 12292
  7.4 0.7 copy-start.9
  8.0 0.7 copy-start.10
  8.7 0.7 copy-start.11
  9.3 52.0 %copy-start.2 = (bf16[1024,1024]{1,0:T(8,128)(2,1)S(1)}, bf16[1024,1024]{1,0:T(8,128)(2,1)}, u32[]{:S(2)}) copy-start(bf16[1024,1024]{1,0:T(8,128)(2,1)} %w_out.1) | copy-start | bytes 6291460
  9.3 52.0 %copy-start.6 = (f32[1024]{0:T(1024)S(1)}, f32[1024]{0:T(1024)}, u32[]{:S(2)}) copy-start(f32[1024]{0:T(1024)} %param.22) | copy-start | bytes 12292

commit v3 on v2

v3 whole, which is shorter than its diff:
```python
import jax
import jax.numpy as jnp
from jax import lax
from jax.experimental import pallas as pl
from jax.experimental.pallas import tpu as pltpu
from jax.sharding import PartitionSpec as P

STRETCH = 128
CHUNK = 256
HALO = 16
ROWS, YS, ZS = 4, 4, 8
MESH = pl.DeviceIdType.MESH
BF16 = jnp.bfloat16
F32 = jnp.float32


def silu(v):
    return v * (0.5 * jnp.tanh(0.5 * v) + 0.5)


def dot(a, b):
    return jnp.dot(a, b, preferred_element_type=F32)


def down_columns(row):
    return jnp.transpose(jnp.broadcast_to(row, (STRETCH, STRETCH)))


def main_kernel(
    lengths_in,
    ids_in,
    pads_in,
    w_dt_in,
    taps_in,
    bias_in,
    rates_in,
    table_in,
    w_in_in,
    w_gate_in,
    carry,
    mix,
    gate,
    outward,
    columns_out,
    lengths,
    ids,
    pads,
    w_dt,
    taps,
    bias,
    rates,
    table,
    w_in,
    w_gate,
    wdt_wide,
    split_steps,
    halo,
    hot,
    projected,
    joined_even,
    joined_odd,
    signal,
    inward,
    in_rows,
    slopes,
    log_rows,
    step_rows,
    tails,
    running,
    states,
    logs,
    row_states,
    row_logs,
    row_before,
    z_out,
    z_states,
    z_before,
    z_log_out,
    z_logs,
    y_out,
    y_states,
    y_log_out,
    y_logs,
    c_out,
    c_states,
    back_out,
    load_sem,
    halo_send,
    halo_recv,
    x_send,
    x_recv,
    xl_send,
    xl_recv,
    z_send,
    z_recv,
    zl_send,
    zl_recv,
    y_send,
    y_recv,
    yl_send,
    yl_recv,
    c_send,
    c_recv,
    b_send,
    b_recv,
):
    users, _, events = ids.shape
    inner = w_gate.shape[1]
    heads = w_dt.shape[0]
    stretches = events // STRETCH
    shares = inner // CHUNK
    part = z_states.shape[2]
    r = lax.axis_index("row")
    col = lax.axis_index("col")
    cols_axis = lax.axis_size("col")
    y, z = col // ZS, lax.rem(col, ZS)
    first = (col * ROWS + r) * events

    loads = []
    pairs = (
        (ids_in, ids),
        (table_in, table),
        (w_dt_in, w_dt),
        (bias_in, bias),
        (rates_in, rates),
        (pads_in, pads),
        (lengths_in, lengths),
        (w_in_in, w_in),
        (taps_in, taps),
        (w_gate_in, w_gate),
    )
    for i, (source, target) in enumerate(pairs):
        loads.append(pltpu.make_async_copy(source, target, load_sem.at[i]))
        loads[-1].start()

    def row_peer(d):
        return lax.rem(r + d, ROWS)

    def z_peer(d):
        return lax.rem(z + d, ZS)

    def to_row(d):
        return {"row": row_peer(d)}

    def to_z(d):
        return {"col": y * ZS + z_peer(d)}

    def to_y(d):
        return {"col": lax.rem(y + d, YS) * ZS + z}

    next_span = {
        "row": row_peer(1),
        "col": lax.rem(col + jnp.where(r == ROWS - 1, 1, 0), cols_axis),
    }
    last_span = {
        "row": row_peer(ROWS - 1),
        "col": lax.rem(col + jnp.where(r == 0, cols_axis - 1, 0), cols_axis),
    }
    barrier = pltpu.get_barrier_semaphore()
    peers = (
        [to_row(d) for d in range(1, ROWS)]
        + [to_z(d) for d in range(1, ZS)]
        + [to_y(d) for d in range(1, YS)]
        + [next_span, last_span]
    )
    for peer in peers:
        pl.semaphore_signal(barrier, inc=1, device_id=peer, device_id_type=MESH)

    sent = []

    def send(src, dst, send_sem, recv_sem, device):
        copy = pltpu.make_async_remote_copy(
            src_ref=src,
            dst_ref=dst,
            send_sem=send_sem,
            recv_sem=recv_sem,
            device_id=device,
            device_id_type=MESH,
        )
        copy.start()
        sent.append(copy)
        return copy

    lanes = lax.broadcasted_iota(jnp.int32, (STRETCH, STRETCH), 1)
    lanes_f = lanes.astype(F32)
    depths = lax.broadcasted_iota(jnp.int32, (STRETCH, STRETCH), 0)
    causal = depths >= lanes

    def one_hot(row, u, begin, rows):
        column = down_columns(row)[STRETCH - rows :, :]
        for j in range(table.shape[0] // STRETCH):
            match = column == lanes_f[:rows] + float(j * STRETCH)
            hot[u, begin : begin + rows, j * STRETCH : (j + 1) * STRETCH] = jnp.where(
                match, 1.0, 0.0
            ).astype(BF16)

    wdt_wide[...] = jnp.zeros_like(wdt_wide)
    loads[0].wait()
    for u in range(users):
        for c in range(stretches):
            row = ids[u, :, c * STRETCH : (c + 1) * STRETCH].astype(F32)
            one_hot(row, u, HALO + c * STRETCH, STRETCH)

    for load in loads[1:7]:
        load.wait()
    wdt_wide[0:heads, :] = w_dt[...]
    raw = lax.dot_general(
        table[...], wdt_wide[...], (((1,), (1,)), ((), ())), preferred_element_type=F32
    )
    raw = raw + jnp.concatenate([bias[...], jnp.zeros((1, STRETCH - heads), F32)], axis=1)
    soft = jnp.maximum(raw, 0.0) + jnp.log1p(jnp.exp(-jnp.abs(raw)))
    high = soft.astype(BF16)
    split_steps[:, 0:STRETCH] = high
    split_steps[:, STRETCH:] = (soft - high.astype(F32)).astype(BF16)
    speed = down_columns(
        jnp.concatenate([rates[...], jnp.zeros((1, STRETCH - heads), F32)], axis=1)
    )[0:heads]
    usable = {}
    for u in range(users):
        picked = dot(hot[u, HALO:, :], split_steps[...])
        step = picked[:, 0:STRETCH] + picked[:, STRETCH:]
        for c in range(stretches):
            place = first + c * STRETCH + lax.broadcasted_iota(jnp.int32, (1, STRETCH), 1)
            rows = slice(c * STRETCH, (c + 1) * STRETCH)
            kept = jnp.logical_and(place < lengths[u], pads[u, :, rows] > 0)
            usable[u, c] = jnp.where(kept, 1.0, 0.0)
            step_t = jnp.transpose(step[rows])[0:heads] * usable[u, c]
            step_rows[u, c] = step_t
            slopes[(u * stretches + c) * heads : (u * stretches + c + 1) * heads, :] = (
                step_t * speed
            )

    pl.semaphore_wait(barrier, len(peers))
    tail = slice(events - STRETCH, events)
    halo_copy = send(ids.at[:, :, tail], halo, halo_send, halo_recv, next_span)

    gained = jnp.dot(
        slopes[...],
        jnp.where(depths <= lanes, 1.0, 0.0),
        preferred_element_type=F32,
        precision=lax.Precision.HIGHEST,
    )
    for u in range(users):
        before = [jnp.zeros((heads, 1), F32)]
        log_t = []
        for c in range(stretches):
            begin = (u * stretches + c) * heads
            log_t.append(gained[begin : begin + heads])
            before.append(before[c] + log_t[c][:, STRETCH - 1 :])
        for c in range(stretches):
            rows = slice(c * STRETCH, (c + 1) * STRETCH)
            log_rows[u, c] = log_t[c]
            so_far = before[c] + log_t[c]
            to_end = jnp.exp(so_far - before[stretches]) * step_rows[u, c]
            for h in range(heads):
                tails[u, h, :, rows] = to_end[h : h + 1, :]
            columns_out[u, rows, :] = jnp.transpose(
                jnp.concatenate(
                    [
                        log_t[c],
                        jnp.broadcast_to(usable[u, c], (heads, STRETCH)),
                        jnp.exp(-so_far),
                        jnp.exp(-log_t[c]),
                        jnp.zeros((STRETCH - 4 * heads, STRETCH), F32),
                    ],
                    axis=0,
                )
            )
        for h in range(heads):
            half = h % 2
            logs[h // 2, u, :, half * STRETCH : (half + 1) * STRETCH] = jnp.broadcast_to(
                before[stretches][h : h + 1, :], (1, STRETCH)
            )
    xl_copies = [
        send(logs.at[row_peer(d)], row_logs.at[r], xl_send.at[d], xl_recv.at[d], to_row(d))
        for d in range(1, ROWS)
    ]
    row_logs[r] = logs[r]

    loads[7].wait()
    loads[8].wait()
    for j in reversed(range(shares + 1)):
        columns = slice(j * CHUNK, (j + 1) * CHUNK)
        projected[:, columns] = dot(table[...], w_in[:, columns]).astype(BF16)

    halo_copy.wait_recv()
    nobody = jnp.logical_and(r == 0, col == 0)
    for u in range(users):
        one_hot(jnp.where(nobody, -1.0, halo[u].astype(F32)), u, 0, HALO)

    joined = (joined_even, joined_odd)

    def gather(u, columns):
        rows = dot(hot[u], projected[:, columns])
        for half in range(2):
            joined[u][half] = rows[:, half * STRETCH : (half + 1) * STRETCH]

    def convolve(u, half, columns):
        total = None
        for k in range(taps.shape[0]):
            begin = HALO - taps.shape[0] + 1 + k
            term = joined[u][half, begin : begin + events, :] * taps[k : k + 1, columns]
            total = term if total is None else total + term
        return total

    for u in range(users):
        gather(u, slice(inner, inner + CHUNK))
    for u in range(users):
        into = convolve(u, 0, slice(inner, inner + STRETCH)).astype(BF16)
        inward[u] = into
        outward[u] = convolve(u, 1, slice(inner + STRETCH, inner + CHUNK)).astype(BF16)
        for c in range(stretches):
            rows = slice(c * STRETCH, (c + 1) * STRETCH)
            in_rows[u, :, rows] = jnp.transpose(into[rows].astype(F32))

    for copy in xl_copies:
        copy.wait_recv()
    block_log = row_logs[0]
    for i in range(1, ROWS):
        block_log = block_log + row_logs[i]
    z_log_out[...] = block_log
    z_logs[z] = block_log
    zl_copies = [
        send(z_log_out, z_logs.at[z], zl_send.at[d], zl_recv.at[d], to_z(d)) for d in range(1, ZS)
    ]

    x_copies = {}
    order = [(d, u) for d in (2, 1, 3, 0) for u in range(users)]

    def share(d, begin=0, size=CHUNK):
        return pl.ds(pl.multiple_of(row_peer(d) * CHUNK + begin, STRETCH), size)

    gather(order[0][1], share(order[0][0]))
    for i, (d, u) in enumerate(order):
        if i + 1 < len(order):
            gather(order[i + 1][1], share(order[i + 1][0]))
        for half in range(2):
            columns = share(d, half * STRETCH, STRETCH)
            values = silu(convolve(u, half, columns)).astype(BF16)
            signal[u, :, columns] = values
            scaled = (in_rows[u] * tails[u, 2 * row_peer(d) + half]).astype(BF16)
            state = dot(scaled, values).astype(BF16)
            cols = slice(half * STRETCH, (half + 1) * STRETCH)
            if d:
                states[u, d, :, cols] = state
            else:
                row_states[u, r, :, cols] = state
        if d:
            x_copies[u, d] = send(
                states.at[u, d],
                row_states.at[u, r],
                x_send.at[u, d],
                x_recv.at[u, d],
                to_row(d),
            )

    for copy in zl_copies:
        copy.wait_recv()
    y_log = z_logs[0]
    for i in range(1, ZS):
        y_log = y_log + z_logs[i]
    y_log_out[...] = y_log
    y_logs[y] = y_log
    yl_copies = [
        send(y_log_out, y_logs.at[y], yl_send.at[d], yl_recv.at[d], to_y(d)) for d in range(1, YS)
    ]

    loads[9].wait()

    def gate_phase(begin, end):
        @pl.loop(begin, end)
        def _(j):
            columns = pl.ds(pl.multiple_of(j * CHUNK, CHUNK), CHUNK)
            opened = dot(table[...], w_gate[:, columns]).astype(BF16)
            opened = silu(opened.astype(F32)).astype(BF16)
            for u in range(users):
                gate[u, :, columns] = dot(hot[u, HALO:, :], opened).astype(BF16)

    def local_phase(u, begin, end):
        @pl.loop(begin, end)
        def _(c):
            rows = pl.ds(pl.multiple_of(c * STRETCH, STRETCH), STRETCH)
            column = columns_out[u, rows, :]
            log_t = log_rows[u, c]
            step_t = step_rows[u, c]
            last = log_t[:, STRETCH - 1 :]
            tail_t = jnp.exp(log_t - last) * step_t
            stay = jnp.exp(-last)
            outs = outward[u, rows, :]
            in_t = in_rows[u, :, rows]
            scores = dot(outs, in_t.astype(BF16))
            for h in range(heads):
                cols = slice(h * STRETCH, (h + 1) * STRETCH)
                gap = jnp.where(causal, log_t[h : h + 1, :] - column[:, h : h + 1], -1e30)
                weights = (scores * jnp.exp(gap) * step_t[h : h + 1, :]).astype(BF16)
                values = signal[u, rows, cols]
                entering = jnp.where(c == 0, 0.0, running[:, cols])
                fade = column[:, 3 * heads + h : 3 * heads + h + 1]
                mix[u, rows, cols] = (
                    dot(weights, values) + dot(outs, entering.astype(BF16)) * fade
                ).astype(BF16)
                scaled = (in_t * tail_t[h : h + 1, :]).astype(BF16)
                running[:, cols] = stay[h : h + 1, :] * entering + dot(scaled, values)

    gate_phase(0, shares // 2)

    for u in range(users):
        for d in range(1, ROWS):
            x_copies[u, d].wait_recv()
        total = row_states[u, 0].astype(F32)
        for i in range(1, ROWS):
            row_before[u, i - 1] = total
            total = jnp.exp(-row_logs[i, u]) * total + row_states[u, i].astype(F32)
        block = total.astype(BF16)
        for k in range(ZS):
            z_out[k, u] = block[k * part : (k + 1) * part]
    z_states[z] = z_out[z]
    z_copies = [
        send(z_out.at[z_peer(d)], z_states.at[z], z_send.at[d], z_recv.at[d], to_z(d))
        for d in (4, 3, 5, 2, 6, 1, 7)
    ]

    gate_phase(shares // 2, shares)
    local_phase(0, 0, 2)

    for copy in z_copies:
        copy.wait_recv()
    total = z_states[0].astype(F32)
    for i in range(1, ZS):
        z_before[i - 1] = total
        total = jnp.exp(-z_logs[i]) * total + z_states[i].astype(F32)
    y_out[...] = total.astype(BF16)
    y_copies = [
        send(y_out, y_states.at[y], y_send.at[d], y_recv.at[d], to_y(d)) for d in (2, 1, 3)
    ]

    local_phase(0, 2, stretches)

    for copy in yl_copies:
        copy.wait_recv()
    for copy in y_copies:
        copy.wait_recv()
    entering = jnp.zeros(y_out.shape, F32)
    for i in range(YS - 1):
        entering = jnp.where(
            i < y, jnp.exp(-y_logs[i]) * entering + y_states[i].astype(F32), entering
        )
    gone = None
    for k in range(ZS):
        value = entering
        if k:
            gone = z_logs[k - 1] if gone is None else gone + z_logs[k - 1]
            value = jnp.exp(-gone) * entering + z_before[k - 1]
        c_out[k] = value.astype(BF16)
    c_states[z] = c_out[z]
    c_copies = [
        send(c_out.at[z_peer(d)], c_states.at[z], c_send.at[d], c_recv.at[d], to_z(d))
        for d in (4, 3, 5, 2, 6, 1, 7)
    ]

    local_phase(1, 0, stretches)

    for copy in c_copies:
        copy.wait_recv()
    gone = [None, row_logs[0]]
    for i in range(2, ROWS):
        gone.append(gone[-1] + row_logs[i - 1])
    for u in range(users):
        for i in range(ROWS):
            for k in range(ZS):
                rows = slice(k * part, (k + 1) * part)
                value = c_states[k, u].astype(F32)
                if i:
                    value = jnp.exp(-gone[i][u]) * value + row_before[u, i - 1, rows, :]
                back_out[u, i, rows, :] = value.astype(BF16)
        carry[u, r] = back_out[u, r]
        for d in (2, 1, 3):
            x_copies[u, -d] = send(
                back_out.at[u, row_peer(d)],
                carry.at[u, r],
                b_send.at[u, d],
                b_recv.at[u, d],
                to_row(d),
            )
    for u in range(users):
        for d in range(1, ROWS):
            x_copies[u, -d].wait_recv()
    for copy in sent:
        copy.wait_send()


def final_kernel(carry, mix, gate, outward, columns_in, gain, w_out, result, gated, normed, done, sems):
    users, events, inner = mix.shape
    heads = inner // STRETCH
    width = w_out.shape[1]

    def norm(u, c):
        rows = slice(c * STRETCH, (c + 1) * STRETCH)
        outs = outward[u, rows, :]
        squares = jnp.zeros((STRETCH, STRETCH), F32)
        for r in range(ROWS):
            carried = dot(outs, carry[u, r])
            for half in range(2):
                h = 2 * r + half
                cols = slice(h * STRETCH, (h + 1) * STRETCH)
                fade = columns_in[u, rows, 2 * heads + h : 2 * heads + h + 1]
                value = fade * carried[:, half * STRETCH : (half + 1) * STRETCH]
                value = value + mix[u, rows, cols].astype(F32)
                value = value * gate[u, rows, cols].astype(F32)
                squares = squares + value * value
                gated[c % 2, :, cols] = value
        mean = jnp.sum(squares, axis=1, keepdims=True) * (1.0 / inner)
        scale = lax.rsqrt(mean + 1.0)
        for h in range(heads):
            cols = slice(h * STRETCH, (h + 1) * STRETCH)
            normed[u, rows, cols] = (gated[c % 2, :, cols] * scale * gain[:, cols]).astype(BF16)

    copies = []

    def project(u, j):
        columns = slice(j * CHUNK, (j + 1) * CHUNK)
        usable = columns_in[u, :, heads : heads + 1]
        done[u, :, columns] = (dot(normed[u], w_out[:, columns]) * usable).astype(BF16)
        return columns

    def store(u, j, columns):
        copy = pltpu.make_async_copy(
            done.at[u, :, columns], result.at[u, 0, :, columns], sems.at[u, j]
        )
        copy.start()
        copies.append(copy)

    blocks = events // STRETCH
    for c in range(blocks):
        norm(0, c)
    for u in range(users):
        for j in range(width // CHUNK):
            columns = project(u, j)
            if u + 1 < users and j < blocks:
                norm(u + 1, j)
            store(u, j, columns)
    for copy in copies:
        copy.wait()


def per_device(
    item_ids,
    pad_masks,
    lengths,
    item_table,
    w_gate,
    w_in,
    w_dt,
    conv_taps,
    dt_bias,
    decay_rates,
    norm_gain,
    w_out,
):
    users, _, events = item_ids.shape
    items, width = item_table.shape
    inner = w_gate.shape[1]
    full = w_in.shape[1]
    heads = decay_rates.shape[0]
    stretches = events // STRETCH
    pair = 2 * STRETCH
    part = STRETCH // ZS
    vmem = pl.BlockSpec(memory_space=pltpu.VMEM)
    hbm = pl.BlockSpec(memory_space=pltpu.HBM)
    dma = pltpu.SemaphoreType.DMA
    carry, mix, gate, outward, decays = pl.pallas_call(
        main_kernel,
        name="main",
        out_shape=(
            jax.ShapeDtypeStruct((users, ROWS, STRETCH, pair), BF16),
            jax.ShapeDtypeStruct((users, events, inner), BF16),
            jax.ShapeDtypeStruct((users, events, inner), BF16),
            jax.ShapeDtypeStruct((users, events, STRETCH), BF16),
            jax.ShapeDtypeStruct((users, events, STRETCH), F32),
        ),
        in_specs=[hbm] * 10,
        out_specs=(vmem,) * 5,
        scratch_shapes=[
            pltpu.SMEM(lengths.shape, lengths.dtype),
            pltpu.VMEM(item_ids.shape, item_ids.dtype),
            pltpu.VMEM(pad_masks.shape, pad_masks.dtype),
            pltpu.VMEM((heads, width), BF16),
            pltpu.VMEM(conv_taps.shape, F32),
            pltpu.VMEM((1, heads), F32),
            pltpu.VMEM((1, heads), F32),
            pltpu.VMEM((items, width), BF16),
            pltpu.VMEM((width, full), BF16),
            pltpu.VMEM((width, inner), BF16),
            pltpu.VMEM((STRETCH, width), BF16),
            pltpu.VMEM((items, 2 * STRETCH), BF16),
            pltpu.VMEM((users, 1, STRETCH), jnp.int32),
            pltpu.VMEM((users, HALO + events, items), BF16),
            pltpu.VMEM((items, full), BF16),
            pltpu.VMEM((2, HALO + events, STRETCH), F32),
            pltpu.VMEM((2, HALO + events, STRETCH), F32),
            pltpu.VMEM((users, events, inner), BF16),
            pltpu.VMEM((users, events, STRETCH), BF16),
            pltpu.VMEM((users, STRETCH, events), F32),
            pltpu.VMEM((users * stretches * heads, STRETCH), F32),
            pltpu.VMEM((users, stretches, heads, STRETCH), F32),
            pltpu.VMEM((users, stretches, heads, STRETCH), F32),
            pltpu.VMEM((users, heads, 1, events), F32),
            pltpu.VMEM((STRETCH, inner), F32),
            pltpu.VMEM((users, ROWS, STRETCH, pair), BF16),
            pltpu.VMEM((ROWS, users, 1, pair), F32),
            pltpu.VMEM((users, ROWS, STRETCH, pair), BF16),
            pltpu.VMEM((ROWS, users, 1, pair), F32),
            pltpu.VMEM((users, ROWS - 1, STRETCH, pair), F32),
            pltpu.VMEM((ZS, users, part, pair), BF16),
            pltpu.VMEM((ZS, users, part, pair), BF16),
            pltpu.VMEM((ZS - 1, users, part, pair), F32),
            pltpu.VMEM((users, 1, pair), F32),
            pltpu.VMEM((ZS, users, 1, pair), F32),
            pltpu.VMEM((users, part, pair), BF16),
            pltpu.VMEM((YS, users, part, pair), BF16),
            pltpu.VMEM((users, 1, pair), F32),
            pltpu.VMEM((YS, users, 1, pair), F32),
            pltpu.VMEM((ZS, users, part, pair), BF16),
            pltpu.VMEM((ZS, users, part, pair), BF16),
            pltpu.VMEM((users, ROWS, STRETCH, pair), BF16),
            dma((10,)),
            dma,
            dma,
        ]
        + [dma((users, ROWS))] * 2
        + [dma((ROWS,))] * 2
        + [dma((ZS,))] * 4
        + [dma((YS,))] * 4
        + [dma((ZS,))] * 2
        + [dma((users, ROWS))] * 2,
        compiler_params=pltpu.CompilerParams(
            collective_id=0, has_side_effects=True, vmem_limit_bytes=36 << 20
        ),
    )(
        *(
            pltpu.with_memory_space_constraint(array, pltpu.HBM)
            for array in (
                lengths,
                item_ids,
                pad_masks,
                w_dt.T,
                conv_taps,
                dt_bias.reshape(1, heads),
                decay_rates.reshape(1, heads),
                item_table,
                w_in,
                w_gate,
            )
        )
    )
    return pl.pallas_call(
        final_kernel,
        name="final",
        out_shape=jax.ShapeDtypeStruct((users, 1, events, w_out.shape[1]), BF16),
        in_specs=[vmem] * 7,
        out_specs=hbm,
        scratch_shapes=[
            pltpu.VMEM((2, STRETCH, inner), F32),
            pltpu.VMEM((users, events, inner), BF16),
            pltpu.VMEM((users, events, w_out.shape[1]), BF16),
            dma((users, w_out.shape[1] // CHUNK)),
        ],
        compiler_params=pltpu.CompilerParams(vmem_limit_bytes=24 << 20),
    )(carry, mix, gate, outward, decays, norm_gain.reshape(1, inner), w_out)


def solution(mesh):
    spans = P("batch", "col", "row")
    return jax.shard_map(
        per_device,
        mesh=mesh,
        in_specs=(spans, spans, P("batch")) + (P(),) * 9,
        out_specs=P("batch", "col", "row", None),
        check_vma=False,
    )
```

time: 67.6 us -> 47.6 us (0.70)
  Pallas kernels: 57.6 us -> 47.4 us
  local copies, waits for them, and re-layouts: 9.34 us -> 0.01 us
    pallas_call x1, Pallas kernels: 52 us -> 42 us  [per_device(): pl.pallas_call(main_kernel, name='main', out_shape=(jax.ShapeDtypeStruct(...]
    unnamed x24 -> x4, local copies, waits for them, and re-layouts: 9.34 us -> 0.01 us
where the time goes in v3:
time: 47.6 us
  Pallas kernels  47.4 us (100%)
    pallas_call x1, Pallas kernels, per_device(): pl.pallas_call(main_kernel, name='main', out_shape=(jax.ShapeDtypeStruct(...  42 us
    pallas_call x1, Pallas kernels, per_device(): pl.pallas_call(final_kernel, name='final', out_shape=jax.ShapeDtypeStruct...  5.34 us

profile of v3, /device:TPU:8, one launch (start us, length us, event | category | flops | bytes accessed | tf_op | source)
XLA Modules:
  0.0 47.6 jit_solution(1740011814696718332)
XLA Ops:
  0.0 0.0 copy-start
  0.0 0.0 copy-start.1
  0.0 42.0 %main.1 = (bf16[2,4,128,256]{3,2,1,0:T(8,128)(2,1)S(1)}, bf16[2,512,1024]{2,1,0:T(8,128)(2,1)S(1)}, bf16[2,512,1024]{2,1,0:T(8,128)(2,1)S(1)}, bf16[2,512,128]{2,1,0:T(8,128)(2,1)S(1)}, f32[2,512,128]{2,1,0:T(8,128)S(1)}) custom-call(s32[2]{0:T(128)} %lengths_in.1, s32[2,1,512]{2,1,0:T(1,128)} %ids_in.1, s32[2,1,512]{2,1,0:T(1,128)} %pads_in.1, ...), custom_call_target="tpu_custom_call" | custom-call | tf_op jit(solution)/shard_map/main/pallas_call | solution.py:571
  42.0 0.0 copy-done
  42.0 0.0 copy-done.1
  42.1 5.3 %final.1 = bf16[2,1,512,1024]{3,2,1,0:T(8,128)(2,1)} custom-call(bf16[2,4,128,256]{3,2,1,0:T(8,128)(2,1)S(1)} %get-tuple-element.10.carry, bf16[2,512,1024]{2,1,0:T(8,128)(2,1)S(1)} %get-tuple-element.11.mix, bf16[2,512,1024]{2,1,0:T(8,128)(2,1)S(1)} %get-tuple-element.12.gate, bf16[2,512,128]{2,1,0:T(8,128)(2,1)S(1)} %get-tuple-element.13.outward, ...), custom_call_target="tpu_custom_call" | custom-call | tf_op jit(solution)/shard_map/final/pallas_call | solution.py:656
Async XLA Ops:
  0.0 42.0 %copy-start = (bf16[1024,1024]{1,0:T(8,128)(2,1)S(1)}, bf16[1024,1024]{1,0:T(8,128)(2,1)}, u32[]{:S(2)}) copy-start(bf16[1024,1024]{1,0:T(8,128)(2,1)} %w_out.1) | copy-start | bytes 6291460
  0.0 42.0 %copy-start.1 = (f32[1024]{0:T(1024)S(1)}, f32[1024]{0:T(1024)}, u32[]{:S(2)}) copy-start(f32[1024]{0:T(1024)} %param.22) | copy-start | bytes 12292

commit v4 on v3

--- a/solution.py
+++ b/solution.py
@@ -14,8 +14,8 @@
 F32 = jnp.float32
 
 
-def silu(v):
-    return v * (0.5 * jnp.tanh(0.5 * v) + 0.5)
+def silu_of_half(v):
+    return v + v * jnp.tanh(v)
 
 
 def dot(a, b):
@@ -37,11 +37,15 @@
     table_in,
     w_in_in,
     w_gate_in,
+    w_out_in,
+    gain_in,
     carry,
     mix,
     gate,
     outward,
     columns_out,
+    total_out,
+    squares,
     lengths,
     ids,
     pads,
@@ -52,6 +56,11 @@
     table,
     w_in,
     w_gate,
+    w_out,
+    gain,
+    half_taps,
+    turned,
+    gated,
     wdt_wide,
     split_steps,
     halo,
@@ -60,7 +69,6 @@
     joined_even,
     joined_odd,
     signal,
-    inward,
     in_rows,
     slopes,
     log_rows,
@@ -85,6 +93,7 @@
     c_states,
     back_out,
     load_sem,
+    near,
     halo_send,
     halo_recv,
     x_send,
@@ -116,8 +125,16 @@
     y, z = col // ZS, lax.rem(col, ZS)
     first = (col * ROWS + r) * events
 
+    def row_peer(d):
+        return lax.rem(r + d, ROWS)
+
+    def share(d, begin=0, size=CHUNK):
+        return pl.ds(pl.multiple_of(row_peer(d) * CHUNK + begin, STRETCH), size)
+
+    shares_order = (2, 1, 3, 0)
+    maps = slice(inner, inner + CHUNK)
     loads = []
-    pairs = (
+    pairs = [
         (ids_in, ids),
         (table_in, table),
         (w_dt_in, w_dt),
@@ -125,16 +142,14 @@
         (rates_in, rates),
         (pads_in, pads),
         (lengths_in, lengths),
-        (w_in_in, w_in),
+        (w_in_in.at[:, maps], w_in.at[:, maps]),
         (taps_in, taps),
-        (w_gate_in, w_gate),
-    )
+    ]
+    pairs += [(w_in_in.at[:, share(d)], w_in.at[:, share(d)]) for d in shares_order]
+    pairs += [(w_gate_in, w_gate), (w_out_in, w_out), (gain_in, gain)]
     for i, (source, target) in enumerate(pairs):
         loads.append(pltpu.make_async_copy(source, target, load_sem.at[i]))
         loads[-1].start()
-
-    def row_peer(d):
-        return lax.rem(r + d, ROWS)
 
     def z_peer(d):
         return lax.rem(z + d, ZS)
@@ -159,13 +174,17 @@
     barrier = pltpu.get_barrier_semaphore()
     peers = (
         [to_row(d) for d in range(1, ROWS)]
-        + [to_z(d) for d in range(1, ZS)]
-        + [to_y(d) for d in range(1, YS)]
         + [next_span, last_span]
+        + [to_z(1), to_z(ZS - 1), to_y(1), to_y(YS - 1)]
     )
     for peer in peers:
         pl.semaphore_signal(barrier, inc=1, device_id=peer, device_id_type=MESH)
 
+    def tell(index, devices):
+        for device in devices:
+            pl.semaphore_signal(near.at[index], inc=1, device_id=device, device_id_type=MESH)
+
+    sides = [to_z(1), to_z(ZS - 1)]
     sent = []
 
     def send(src, dst, send_sem, recv_sem, device):
@@ -212,6 +231,11 @@
     high = soft.astype(BF16)
     split_steps[:, 0:STRETCH] = high
     split_steps[:, STRETCH:] = (soft - high.astype(F32)).astype(BF16)
+    pl.semaphore_wait(barrier, len(peers))
+    tail = slice(events - STRETCH, events)
+    halo_copy = send(ids.at[:, :, tail], halo, halo_send, halo_recv, next_span)
+    tell(0, sides)
+    tell(3, [to_y(1), to_y(YS - 1)])
     speed = down_columns(
         jnp.concatenate([rates[...], jnp.zeros((1, STRETCH - heads), F32)], axis=1)
     )[0:heads]
@@ -229,10 +253,6 @@
             slopes[(u * stretches + c) * heads : (u * stretches + c + 1) * heads, :] = (
                 step_t * speed
             )
-
-    pl.semaphore_wait(barrier, len(peers))
-    tail = slice(events - STRETCH, events)
-    halo_copy = send(ids.at[:, :, tail], halo, halo_send, halo_recv, next_span)
 
     gained = jnp.dot(
         slopes[...],
@@ -254,12 +274,15 @@
             to_end = jnp.exp(so_far - before[stretches]) * step_rows[u, c]
             for h in range(heads):
                 tails[u, h, :, rows] = to_end[h : h + 1, :]
+            left = jnp.exp(-so_far)
+            turned[u, c, 0:heads, :] = left
+            turned[u, c, heads:, :] = left
             columns_out[u, rows, :] = jnp.transpose(
                 jnp.concatenate(
                     [
                         log_t[c],
                         jnp.broadcast_to(usable[u, c], (heads, STRETCH)),
-                        jnp.exp(-so_far),
+                        turned[u, c, pl.ds(2 * r, heads), :],
                         jnp.exp(-log_t[c]),
                         jnp.zeros((STRETCH - 4 * heads, STRETCH), F32),
                     ],
@@ -271,6 +294,8 @@
             logs[h // 2, u, :, half * STRETCH : (half + 1) * STRETCH] = jnp.broadcast_to(
                 before[stretches][h : h + 1, :], (1, STRETCH)
             )
+    pl.semaphore_wait(near.at[0], 2)
+    tell(1, sides)
     xl_copies = [
         send(logs.at[row_peer(d)], row_logs.at[r], xl_send.at[d], xl_recv.at[d], to_row(d))
         for d in range(1, ROWS)
@@ -279,9 +304,16 @@
 
     loads[7].wait()
     loads[8].wait()
-    for j in reversed(range(shares + 1)):
-        columns = slice(j * CHUNK, (j + 1) * CHUNK)
-        projected[:, columns] = dot(table[...], w_in[:, columns]).astype(BF16)
+    half_taps[...] = 0.5 * taps[...]
+
+    def project(slot, columns):
+        projected[slot] = dot(table[...], w_in[:, columns]).astype(BF16)
+
+    project(ROWS, maps)
+    loads[9].wait()
+    project(2, share(2))
+    pl.semaphore_wait(near.at[1], 2)
+    tell(2, sides)
 
     halo_copy.wait_recv()
     nobody = jnp.logical_and(r == 0, col == 0)
@@ -290,53 +322,39 @@
 
     joined = (joined_even, joined_odd)
 
-    def gather(u, columns):
-        rows = dot(hot[u], projected[:, columns])
+    def gather(u, slot):
+        rows = dot(hot[u], projected[slot])
         for half in range(2):
             joined[u][half] = rows[:, half * STRETCH : (half + 1) * STRETCH]
 
-    def convolve(u, half, columns):
+    def convolve(u, half, weights, columns):
         total = None
-        for k in range(taps.shape[0]):
-            begin = HALO - taps.shape[0] + 1 + k
-            term = joined[u][half, begin : begin + events, :] * taps[k : k + 1, columns]
+        for k in range(weights.shape[0]):
+            begin = HALO - weights.shape[0] + 1 + k
+            term = joined[u][half, begin : begin + events, :] * weights[k : k + 1, columns]
             total = term if total is None else total + term
         return total
 
     for u in range(users):
-        gather(u, slice(inner, inner + CHUNK))
-    for u in range(users):
-        into = convolve(u, 0, slice(inner, inner + STRETCH)).astype(BF16)
-        inward[u] = into
-        outward[u] = convolve(u, 1, slice(inner + STRETCH, inner + CHUNK)).astype(BF16)
+        gather(u, ROWS)
+    for u in range(users):
+        into = convolve(u, 0, taps, slice(inner, inner + STRETCH)).astype(BF16)
+        outs = convolve(u, 1, taps, slice(inner + STRETCH, inner + CHUNK))
+        outward[u] = outs.astype(BF16)
         for c in range(stretches):
             rows = slice(c * STRETCH, (c + 1) * STRETCH)
             in_rows[u, :, rows] = jnp.transpose(into[rows].astype(F32))
 
-    for copy in xl_copies:
-        copy.wait_recv()
-    block_log = row_logs[0]
-    for i in range(1, ROWS):
-        block_log = block_log + row_logs[i]
-    z_log_out[...] = block_log
-    z_logs[z] = block_log
-    zl_copies = [
-        send(z_log_out, z_logs.at[z], zl_send.at[d], zl_recv.at[d], to_z(d)) for d in range(1, ZS)
-    ]
-
     x_copies = {}
-    order = [(d, u) for d in (2, 1, 3, 0) for u in range(users)]
-
-    def share(d, begin=0, size=CHUNK):
-        return pl.ds(pl.multiple_of(row_peer(d) * CHUNK + begin, STRETCH), size)
-
-    gather(order[0][1], share(order[0][0]))
-    for i, (d, u) in enumerate(order):
+    order = [(d, u) for d in shares_order for u in range(users)]
+
+    def state_step(i):
+        d, u = order[i]
         if i + 1 < len(order):
-            gather(order[i + 1][1], share(order[i + 1][0]))
+            gather(order[i + 1][1], order[i + 1][0])
         for half in range(2):
             columns = share(d, half * STRETCH, STRETCH)
-            values = silu(convolve(u, half, columns)).astype(BF16)
+            values = silu_of_half(convolve(u, half, half_taps, columns)).astype(BF16)
             signal[u, :, columns] = values
             scaled = (in_rows[u] * tails[u, 2 * row_peer(d) + half]).astype(BF16)
             state = dot(scaled, values).astype(BF16)
@@ -354,6 +372,32 @@
                 to_row(d),
             )
 
+    gather(order[0][1], 2)
+    state_step(0)
+    for load in loads[10:13]:
+        load.wait()
+    project(1, share(1))
+    state_step(1)
+    project(3, share(3))
+    state_step(2)
+
+    for copy in xl_copies:
+        copy.wait_recv()
+    block_log = row_logs[0]
+    for i in range(1, ROWS):
+        block_log = block_log + row_logs[i]
+    z_log_out[...] = block_log
+    z_logs[z] = block_log
+    pl.semaphore_wait(near.at[2], 2)
+    pl.semaphore_wait(near.at[3], 2)
+    zl_copies = [
+        send(z_log_out, z_logs.at[z], zl_send.at[d], zl_recv.at[d], to_z(d)) for d in range(1, ZS)
+    ]
+
+    project(0, share(0))
+    for i in range(3, len(order)):
+        state_step(i)
+
     for copy in zl_copies:
         copy.wait_recv()
     y_log = z_logs[0]
@@ -365,14 +409,14 @@
         send(y_log_out, y_logs.at[y], yl_send.at[d], yl_recv.at[d], to_y(d)) for d in range(1, YS)
     ]
 
-    loads[9].wait()
+    loads[13].wait()
 
     def gate_phase(begin, end):
         @pl.loop(begin, end)
         def _(j):
             columns = pl.ds(pl.multiple_of(j * CHUNK, CHUNK), CHUNK)
             opened = dot(table[...], w_gate[:, columns]).astype(BF16)
-            opened = silu(opened.astype(F32)).astype(BF16)
+            opened = silu_of_half(0.5 * opened.astype(F32)).astype(BF16)
             for u in range(users):
                 gate[u, :, columns] = dot(hot[u, HALO:, :], opened).astype(BF16)
 
@@ -482,63 +526,96 @@
                 b_recv.at[u, d],
                 to_row(d),
             )
-    for u in range(users):
-        for d in range(1, ROWS):
+    for load in loads[14:]:
+        load.wait()
+
+    def share_step(u, d):
+        for c in range(stretches):
+            rows = slice(c * STRETCH, (c + 1) * STRETCH)
+            carried = dot(outward[u, rows, :], carry[u, row_peer(d)])
+            both = None
+            for half in range(2):
+                cols = share(d, half * STRETCH, STRETCH)
+                place = 2 * heads + 2 * d + half
+                value = (
+                    columns_out[u, rows, place : place + 1]
+                    * carried[:, half * STRETCH : (half + 1) * STRETCH]
+                    + mix[u, rows, cols].astype(F32)
+                ) * gate[u, rows, cols].astype(F32)
+                gated[rows, half * STRETCH : (half + 1) * STRETCH] = (
+                    value * gain[:, cols]
+                ).astype(BF16)
+                both = value * value if both is None else both + value * value
+            squares[u, rows, :] = squares[u, rows, :] + both if d else both
+        for j in range(w_out.shape[1] // CHUNK):
+            columns = slice(j * CHUNK, (j + 1) * CHUNK)
+            term = dot(gated[...], w_out[share(d), columns])
+            total_out[u, :, columns] = total_out[u, :, columns] + term if d else term
+
+    for u in range(users):
+        share_step(u, 0)
+    for u in range(users):
+        for d in (1, 3) if u + 1 == users else (1, 3, 2):
             x_copies[u, -d].wait_recv()
+            share_step(u, ROWS - d)
+    x_copies[users - 1, -2].wait_recv()
     for copy in sent:
         copy.wait_send()
 
 
-def final_kernel(carry, mix, gate, outward, columns_in, gain, w_out, result, gated, normed, done, sems):
+def final_kernel(
+    carry, mix, gate, outward, columns_in, totals, squares, gain, w_out, result, gated, done, sems
+):
     users, events, inner = mix.shape
     heads = inner // STRETCH
     width = w_out.shape[1]
-
-    def norm(u, c):
-        rows = slice(c * STRETCH, (c + 1) * STRETCH)
-        outs = outward[u, rows, :]
-        squares = jnp.zeros((STRETCH, STRETCH), F32)
-        for r in range(ROWS):
-            carried = dot(outs, carry[u, r])
-            for half in range(2):
-                h = 2 * r + half
-                cols = slice(h * STRETCH, (h + 1) * STRETCH)
-                fade = columns_in[u, rows, 2 * heads + h : 2 * heads + h + 1]
-                value = fade * carried[:, half * STRETCH : (half + 1) * STRETCH]
-                value = value + mix[u, rows, cols].astype(F32)
-                value = value * gate[u, rows, cols].astype(F32)
-                squares = squares + value * value
-                gated[c % 2, :, cols] = value
-        mean = jnp.sum(squares, axis=1, keepdims=True) * (1.0 / inner)
-        scale = lax.rsqrt(mean + 1.0)
-        for h in range(heads):
-            cols = slice(h * STRETCH, (h + 1) * STRETCH)
-            normed[u, rows, cols] = (gated[c % 2, :, cols] * scale * gain[:, cols]).astype(BF16)
-
+    last = users - 1
+    owner = lax.rem(lax.axis_index("row") + 2, ROWS)
     copies = []
-
-    def project(u, j):
+    scale = {}
+
+    def scale_of(u, more):
+        total = squares[u] if more is None else squares[u] + more
+        mean = jnp.sum(total, axis=1, keepdims=True) * (1.0 / inner)
+        return lax.rsqrt(mean + 1.0) * columns_in[u, :, heads : heads + 1]
+
+    def store(u, j, values):
         columns = slice(j * CHUNK, (j + 1) * CHUNK)
-        usable = columns_in[u, :, heads : heads + 1]
-        done[u, :, columns] = (dot(normed[u], w_out[:, columns]) * usable).astype(BF16)
-        return columns
-
-    def store(u, j, columns):
+        done[u, :, columns] = (values * scale[u]).astype(BF16)
         copy = pltpu.make_async_copy(
             done.at[u, :, columns], result.at[u, 0, :, columns], sems.at[u, j]
         )
         copy.start()
         copies.append(copy)
 
-    blocks = events // STRETCH
-    for c in range(blocks):
-        norm(0, c)
+    both = []
+    for c in range(events // STRETCH):
+        rows = slice(c * STRETCH, (c + 1) * STRETCH)
+        carried = dot(outward[last, rows, :], carry[last, owner])
+        added = None
+        for half in range(2):
+            cols = pl.ds(pl.multiple_of(owner * CHUNK + half * STRETCH, STRETCH), STRETCH)
+            place = 2 * heads + 2 * 2 + half
+            value = (
+                columns_in[last, rows, place : place + 1]
+                * carried[:, half * STRETCH : (half + 1) * STRETCH]
+                + mix[last, rows, cols].astype(F32)
+            ) * gate[last, rows, cols].astype(F32)
+            gated[rows, half * STRETCH : (half + 1) * STRETCH] = (value * gain[:, cols]).astype(
+                BF16
+            )
+            added = value * value if added is None else added + value * value
+        both.append(added)
+    for u in range(users):
+        scale[u] = scale_of(u, jnp.concatenate(both, axis=0) if u == last else None)
     for u in range(users):
         for j in range(width // CHUNK):
-            columns = project(u, j)
-            if u + 1 < users and j < blocks:
-                norm(u + 1, j)
-            store(u, j, columns)
+            columns = slice(j * CHUNK, (j + 1) * CHUNK)
+            values = totals[u, :, columns]
+            if u == last:
+                rows = pl.ds(pl.multiple_of(owner * CHUNK, CHUNK), CHUNK)
+                values = values + dot(gated[...], w_out[rows, columns])
+            store(u, j, values)
     for copy in copies:
         copy.wait()
 
@@ -568,7 +645,7 @@
     vmem = pl.BlockSpec(memory_space=pltpu.VMEM)
     hbm = pl.BlockSpec(memory_space=pltpu.HBM)
     dma = pltpu.SemaphoreType.DMA
-    carry, mix, gate, outward, decays = pl.pallas_call(
+    carry, mix, gate, outward, columns, totals, squares = pl.pallas_call(
         main_kernel,
         name="main",
         out_shape=(
@@ -577,9 +654,11 @@
             jax.ShapeDtypeStruct((users, events, inner), BF16),
             jax.ShapeDtypeStruct((users, events, STRETCH), BF16),
             jax.ShapeDtypeStruct((users, events, STRETCH), F32),
+            jax.ShapeDtypeStruct((users, events, w_out.shape[1]), F32),
+            jax.ShapeDtypeStruct((users, events, STRETCH), F32),
         ),
-        in_specs=[hbm] * 10,
-        out_specs=(vmem,) * 5,
+        in_specs=[hbm] * 12,
+        out_specs=(vmem,) * 7,
         scratch_shapes=[
             pltpu.SMEM(lengths.shape, lengths.dtype),
             pltpu.VMEM(item_ids.shape, item_ids.dtype),
@@ -591,15 +670,19 @@
             pltpu.VMEM((items, width), BF16),
             pltpu.VMEM((width, full), BF16),
             pltpu.VMEM((width, inner), BF16),
+            pltpu.VMEM(w_out.shape, BF16),
+            pltpu.VMEM((1, inner), F32),
+            pltpu.VMEM(conv_taps.shape, F32),
+            pltpu.VMEM((users, stretches, 2 * heads, STRETCH), F32),
+            pltpu.VMEM((events, CHUNK), BF16),
             pltpu.VMEM((STRETCH, width), BF16),
             pltpu.VMEM((items, 2 * STRETCH), BF16),
             pltpu.VMEM((users, 1, STRETCH), jnp.int32),
             pltpu.VMEM((users, HALO + events, items), BF16),
-            pltpu.VMEM((items, full), BF16),
+            pltpu.VMEM((ROWS + 1, items, CHUNK), BF16),
             pltpu.VMEM((2, HALO + events, STRETCH), F32),
             pltpu.VMEM((2, HALO + events, STRETCH), F32),
             pltpu.VMEM((users, events, inner), BF16),
-            pltpu.VMEM((users, events, STRETCH), BF16),
             pltpu.VMEM((users, STRETCH, events), F32),
             pltpu.VMEM((users * stretches * heads, STRETCH), F32),
             pltpu.VMEM((users, stretches, heads, STRETCH), F32),
@@ -623,7 +706,8 @@
             pltpu.VMEM((ZS, users, part, pair), BF16),
             pltpu.VMEM((ZS, users, part, pair), BF16),
             pltpu.VMEM((users, ROWS, STRETCH, pair), BF16),
-            dma((10,)),
+            dma((16,)),
+            pltpu.SemaphoreType.REGULAR((4,)),
             dma,
             dma,
         ]
@@ -650,6 +734,8 @@
                 item_table,
                 w_in,
                 w_gate,
+                w_out,
+                norm_gain.reshape(1, inner),
             )
         )
     )
@@ -657,16 +743,15 @@
         final_kernel,
         name="final",
         out_shape=jax.ShapeDtypeStruct((users, 1, events, w_out.shape[1]), BF16),
-        in_specs=[vmem] * 7,
+        in_specs=[vmem] * 9,
         out_specs=hbm,
         scratch_shapes=[
-            pltpu.VMEM((2, STRETCH, inner), F32),
-            pltpu.VMEM((users, events, inner), BF16),
+            pltpu.VMEM((events, CHUNK), BF16),
             pltpu.VMEM((users, events, w_out.shape[1]), BF16),
             dma((users, w_out.shape[1] // CHUNK)),
         ],
-        compiler_params=pltpu.CompilerParams(vmem_limit_bytes=24 << 20),
-    )(carry, mix, gate, outward, decays, norm_gain.reshape(1, inner), w_out)
+        compiler_params=pltpu.CompilerParams(vmem_limit_bytes=16 << 20),
+    )(carry, mix, gate, outward, columns, totals, squares, norm_gain.reshape(1, inner), w_out)
 
 
 def solution(mesh):

time: 47.6 us -> 47.1 us (0.989); the launches traced: 47.6 us -> 46.6 us
  Pallas kernels: 47.4 us -> 46.4 us
    pallas_call x1, Pallas kernels: 5.34 us -> 2.21 us  [per_device(): pl.pallas_call(final_kernel, name='final', out_shape=jax.ShapeDtypeStruct...]
    pallas_call x1, Pallas kernels: 42 us -> 44.2 us  [per_device(): pl.pallas_call(main_kernel, name='main', out_shape=(jax.ShapeDtypeStruct(...]
where the time goes in v4:
time: 47.1 us; the launch traced here: 46.6 us
  Pallas kernels  46.4 us (99%)
    pallas_call x1, Pallas kernels, per_device(): pl.pallas_call(main_kernel, name='main', out_shape=(jax.ShapeDtypeStruct(...  44.2 us
    pallas_call x1, Pallas kernels, per_device(): pl.pallas_call(final_kernel, name='final', out_shape=jax.ShapeDtypeStruct...  2.21 us

profile of v4, /device:TPU:8, one launch (start us, length us, event | category | flops | bytes accessed | tf_op | source)
XLA Modules:
  0.0 46.6 jit_solution(6014582419505970295)
XLA Ops:
  0.0 0.0 copy-start
  0.0 0.0 copy-start.1
  0.0 44.2 %main.1 = (bf16[2,4,128,256]{3,2,1,0:T(8,128)(2,1)S(1)}, bf16[2,512,1024]{2,1,0:T(8,128)(2,1)S(1)}, bf16[2,512,1024]{2,1,0:T(8,128)(2,1)S(1)}, bf16[2,512,128]{2...) custom-call(s32[2]{0:T(128)} %lengths_in.1, ...), custom_call_target="tpu_custom_call" | custom-call | tf_op jit(solution)/shard_map/main/pallas_call | solution.py:648
  44.2 0.0 copy-done
  44.2 0.0 copy-done.1
  44.2 2.2 %final.1 = bf16[2,1,512,1024]{3,2,1,0:T(8,128)(2,1)} custom-call(bf16[2,4,128,256]{3,2,1,0:T(8,128)(2,1)S(1)} %get-tuple-element.12.carry, bf16[2,512,1024]{2,1,0:T(8,128)(2,1)S(1)} %get-tuple-element.13.mix, bf16[2,512,1024]{2,1,0:T(8,128)(2,1)S(1)} %get-tuple-element.14.gate, bf16[2,512,128]{2,1,0:T(8,128)(2,1)S(1)} %get-tuple-element.15.outward, ...), custom_call_target="tpu_custom_call" | custom-call | tf_op jit(solution)/shard_map/final/pallas_call | solution.py:742
Async XLA Ops:
  0.0 44.2 %copy-start = (bf16[1024,1024]{1,0:T(8,128)(2,1)S(1)}, bf16[1024,1024]{1,0:T(8,128)(2,1)}, u32[]{:S(2)}) copy-start(bf16[1024,1024]{1,0:T(8,128)(2,1)} %w_out.1) | copy-start | bytes 6291460
  0.0 44.2 %copy-start.1 = (f32[1024]{0:T(1024)S(1)}, f32[1024]{0:T(1024)}, u32[]{:S(2)}) copy-start(f32[1024]{0:T(1024)} %param.22) | copy-start | bytes 12292

commit v5 on v4

--- a/solution.py
+++ b/solution.py
@@ -146,7 +146,7 @@
         (taps_in, taps),
     ]
     pairs += [(w_in_in.at[:, share(d)], w_in.at[:, share(d)]) for d in shares_order]
-    pairs += [(w_gate_in, w_gate), (w_out_in, w_out), (gain_in, gain)]
+    pairs += [(w_gate_in, w_gate), (w_out_in.at[share(0)], w_out), (gain_in, gain)]
     for i, (source, target) in enumerate(pairs):
         loads.append(pltpu.make_async_copy(source, target, load_sem.at[i]))
         loads[-1].start()
@@ -236,6 +236,15 @@
     halo_copy = send(ids.at[:, :, tail], halo, halo_send, halo_recv, next_span)
     tell(0, sides)
     tell(3, [to_y(1), to_y(YS - 1)])
+    for load in loads[7:10]:
+        load.wait()
+    half_taps[...] = 0.5 * taps[...]
+
+    def project(slot, columns):
+        projected[slot] = dot(table[...], w_in[:, columns]).astype(BF16)
+
+    project(ROWS, maps)
+    project(2, share(2))
     speed = down_columns(
         jnp.concatenate([rates[...], jnp.zeros((1, STRETCH - heads), F32)], axis=1)
     )[0:heads]
@@ -302,19 +311,6 @@
     ]
     row_logs[r] = logs[r]
 
-    loads[7].wait()
-    loads[8].wait()
-    half_taps[...] = 0.5 * taps[...]
-
-    def project(slot, columns):
-        projected[slot] = dot(table[...], w_in[:, columns]).astype(BF16)
-
-    project(ROWS, maps)
-    loads[9].wait()
-    project(2, share(2))
-    pl.semaphore_wait(near.at[1], 2)
-    tell(2, sides)
-
     halo_copy.wait_recv()
     nobody = jnp.logical_and(r == 0, col == 0)
     for u in range(users):
@@ -335,9 +331,7 @@
             total = term if total is None else total + term
         return total
 
-    for u in range(users):
-        gather(u, ROWS)
-    for u in range(users):
+    def make_maps(u):
         into = convolve(u, 0, taps, slice(inner, inner + STRETCH)).astype(BF16)
         outs = convolve(u, 1, taps, slice(inner + STRETCH, inner + CHUNK))
         outward[u] = outs.astype(BF16)
@@ -348,9 +342,9 @@
     x_copies = {}
     order = [(d, u) for d in shares_order for u in range(users)]
 
-    def state_step(i):
+    def state_step(i, prefetch=True):
         d, u = order[i]
-        if i + 1 < len(order):
+        if prefetch and i + 1 < len(order):
             gather(order[i + 1][1], order[i + 1][0])
         for half in range(2):
             columns = share(d, half * STRETCH, STRETCH)
@@ -372,10 +366,16 @@
                 to_row(d),
             )
 
-    gather(order[0][1], 2)
+    gather(0, ROWS)
+    gather(1, ROWS)
+    make_maps(0)
+    gather(0, 2)
+    make_maps(1)
     state_step(0)
     for load in loads[10:13]:
         load.wait()
+    pl.semaphore_wait(near.at[1], 2)
+    tell(2, sides)
     project(1, share(1))
     state_step(1)
     project(3, share(3))
@@ -453,7 +453,8 @@
             x_copies[u, d].wait_recv()
         total = row_states[u, 0].astype(F32)
         for i in range(1, ROWS):
-            row_before[u, i - 1] = total
+            for k in range(ZS):
+                row_before[i - 1, k, u] = total[k * part : (k + 1) * part]
             total = jnp.exp(-row_logs[i, u]) * total + row_states[u, i].astype(F32)
         block = total.astype(BF16)
         for k in range(ZS):
@@ -497,46 +498,56 @@
             value = jnp.exp(-gone) * entering + z_before[k - 1]
         c_out[k] = value.astype(BF16)
     c_states[z] = c_out[z]
-    c_copies = [
-        send(c_out.at[z_peer(d)], c_states.at[z], c_send.at[d], c_recv.at[d], to_z(d))
+    c_copies = {
+        d: send(c_out.at[z_peer(d)], c_states.at[z], c_send.at[d], c_recv.at[d], to_z(d))
         for d in (4, 3, 5, 2, 6, 1, 7)
-    ]
-
-    local_phase(1, 0, stretches)
-
-    for copy in c_copies:
-        copy.wait_recv()
+    }
+
     gone = [None, row_logs[0]]
     for i in range(2, ROWS):
         gone.append(gone[-1] + row_logs[i - 1])
-    for u in range(users):
-        for i in range(ROWS):
-            for k in range(ZS):
-                rows = slice(k * part, (k + 1) * part)
-                value = c_states[k, u].astype(F32)
-                if i:
-                    value = jnp.exp(-gone[i][u]) * value + row_before[u, i - 1, rows, :]
-                back_out[u, i, rows, :] = value.astype(BF16)
-        carry[u, r] = back_out[u, r]
-        for d in (2, 1, 3):
-            x_copies[u, -d] = send(
-                back_out.at[u, row_peer(d)],
-                carry.at[u, r],
-                b_send.at[u, d],
-                b_recv.at[u, d],
-                to_row(d),
+    kept = [None] + [jnp.exp(-gone[i]) for i in range(1, ROWS)]
+    b_copies = []
+
+    def forward(d):
+        k = z_peer(ZS - d)
+        value = c_states[k].astype(F32)
+        back_out[0, k] = c_states[k]
+        for i in range(1, ROWS):
+            back_out[i, k] = (kept[i] * value + row_before[i - 1, k]).astype(BF16)
+        carry[r, k] = back_out[r, k]
+        for x in (2, 1, 3):
+            b_copies.append(
+                send(
+                    back_out.at[row_peer(x), k],
+                    carry.at[r, k],
+                    b_send.at[x, d],
+                    b_recv.at[x, d],
+                    to_row(x),
+                )
             )
+
+    forward(0)
+    local_phase(1, 0, 2)
+    for begin, ends in ((2, (1, 7)), (3, (2, 6)), (4, (3, 5, 4))):
+        for d in ends:
+            c_copies[d].wait_recv()
+            forward(d)
+        if begin < stretches:
+            local_phase(1, begin, begin + 1)
+
     for load in loads[14:]:
         load.wait()
 
-    def share_step(u, d):
+    for u in range(users):
+        held = carry[r, :, u].reshape(STRETCH, CHUNK)
         for c in range(stretches):
             rows = slice(c * STRETCH, (c + 1) * STRETCH)
-            carried = dot(outward[u, rows, :], carry[u, row_peer(d)])
+            carried = dot(outward[u, rows, :], held)
             both = None
             for half in range(2):
-                cols = share(d, half * STRETCH, STRETCH)
-                place = 2 * heads + 2 * d + half
+                cols = share(0, half * STRETCH, STRETCH)
+                place = 2 * heads + half
                 value = (
                     columns_out[u, rows, place : place + 1]
                     * carried[:, half * STRETCH : (half + 1) * STRETCH]
@@ -546,76 +557,95 @@
                     value * gain[:, cols]
                 ).astype(BF16)
                 both = value * value if both is None else both + value * value
-            squares[u, rows, :] = squares[u, rows, :] + both if d else both
+            squares[u, rows, :] = both
         for j in range(w_out.shape[1] // CHUNK):
             columns = slice(j * CHUNK, (j + 1) * CHUNK)
-            term = dot(gated[...], w_out[share(d), columns])
-            total_out[u, :, columns] = total_out[u, :, columns] + term if d else term
-
-    for u in range(users):
-        share_step(u, 0)
-    for u in range(users):
-        for d in (1, 3) if u + 1 == users else (1, 3, 2):
-            x_copies[u, -d].wait_recv()
-            share_step(u, ROWS - d)
-    x_copies[users - 1, -2].wait_recv()
+            total_out[u, :, columns] = dot(gated[...], w_out[:, columns])
+    for copy in b_copies:
+        copy.wait_recv()
     for copy in sent:
         copy.wait_send()
 
 
 def final_kernel(
-    carry, mix, gate, outward, columns_in, totals, squares, gain, w_out, result, gated, done, sems
+    carry,
+    mix,
+    gate,
+    outward,
+    columns_in,
+    totals,
+    partial,
+    gain,
+    w_out,
+    result,
+    gated,
+    squares,
+    done,
+    sems,
 ):
     users, events, inner = mix.shape
     heads = inner // STRETCH
     width = w_out.shape[1]
-    last = users - 1
-    owner = lax.rem(lax.axis_index("row") + 2, ROWS)
+    block = 2 * STRETCH
     copies = []
     scale = {}
 
-    def scale_of(u, more):
-        total = squares[u] if more is None else squares[u] + more
-        mean = jnp.sum(total, axis=1, keepdims=True) * (1.0 / inner)
-        return lax.rsqrt(mean + 1.0) * columns_in[u, :, heads : heads + 1]
-
-    def store(u, j, values):
+    def owner(d, begin=0, size=CHUNK):
+        place = lax.rem(lax.axis_index("row") + d, ROWS) * CHUNK + begin
+        return pl.ds(pl.multiple_of(place, STRETCH), size)
+
+    def open_gate(u, c, d):
+        rows = slice(c * block, (c + 1) * block)
+        held = carry[lax.rem(lax.axis_index("row") + d, ROWS), :, u].reshape(STRETCH, CHUNK)
+        carried = dot(outward[u, rows, :], held)
+        added = None
+        for half in range(2):
+            cols = owner(d, half * STRETCH, STRETCH)
+            place = 2 * heads + 2 * d + half
+            value = (
+                columns_in[u, rows, place : place + 1]
+                * carried[:, half * STRETCH : (half + 1) * STRETCH]
+                + mix[u, rows, cols].astype(F32)
+            ) * gate[u, rows, cols].astype(F32)
+            begin = (d - 1) * CHUNK + half * STRETCH
+            gated[u, rows, begin : begin + STRETCH] = (value * gain[:, cols]).astype(BF16)
+            added = value * value if added is None else added + value * value
+        before = partial if d == 1 else squares
+        squares[u, rows, :] = before[u, rows, :] + added
+
+    def scale_of(u):
+        mean = jnp.sum(squares[u], axis=1, keepdims=True) * (1.0 / inner)
+        scale[u] = lax.rsqrt(mean + 1.0) * columns_in[u, :, heads : heads + 1]
+
+    def project(u, j):
         columns = slice(j * CHUNK, (j + 1) * CHUNK)
+        values = totals[u, :, columns]
+        for d in range(1, ROWS):
+            values = values + dot(
+                gated[u, :, (d - 1) * CHUNK : d * CHUNK], w_out[owner(d), columns]
+            )
         done[u, :, columns] = (values * scale[u]).astype(BF16)
+
+    def store(u, j):
+        columns = slice(j * CHUNK, (j + 1) * CHUNK)
         copy = pltpu.make_async_copy(
             done.at[u, :, columns], result.at[u, 0, :, columns], sems.at[u, j]
         )
         copy.start()
         copies.append(copy)
 
-    both = []
-    for c in range(events // STRETCH):
-        rows = slice(c * STRETCH, (c + 1) * STRETCH)
-        carried = dot(outward[last, rows, :], carry[last, owner])
-        added = None
-        for half in range(2):
-            cols = pl.ds(pl.multiple_of(owner * CHUNK + half * STRETCH, STRETCH), STRETCH)
-            place = 2 * heads + 2 * 2 + half
-            value = (
-                columns_in[last, rows, place : place + 1]
-                * carried[:, half * STRETCH : (half + 1) * STRETCH]
-                + mix[last, rows, cols].astype(F32)
-            ) * gate[last, rows, cols].astype(F32)
-            gated[rows, half * STRETCH : (half + 1) * STRETCH] = (value * gain[:, cols]).astype(
-                BF16
-            )
-            added = value * value if added is None else added + value * value
-        both.append(added)
+    steps = [(c, d) for c in range(events // block) for d in range(1, ROWS)]
+    for c, d in steps:
+        open_gate(0, c, d)
     for u in range(users):
-        scale[u] = scale_of(u, jnp.concatenate(both, axis=0) if u == last else None)
-    for u in range(users):
+        scale_of(u)
+        left = list(steps)
         for j in range(width // CHUNK):
-            columns = slice(j * CHUNK, (j + 1) * CHUNK)
-            values = totals[u, :, columns]
-            if u == last:
-                rows = pl.ds(pl.multiple_of(owner * CHUNK, CHUNK), CHUNK)
-                values = values + dot(gated[...], w_out[rows, columns])
-            store(u, j, values)
+            project(u, j)
+            for _ in range(2):
+                if u + 1 < users and left:
+                    open_gate(u + 1, *left.pop(0))
+            store(u, j)
     for copy in copies:
         copy.wait()
 
@@ -649,7 +679,7 @@
         main_kernel,
         name="main",
         out_shape=(
-            jax.ShapeDtypeStruct((users, ROWS, STRETCH, pair), BF16),
+            jax.ShapeDtypeStruct((ROWS, ZS, users, part, pair), BF16),
             jax.ShapeDtypeStruct((users, events, inner), BF16),
             jax.ShapeDtypeStruct((users, events, inner), BF16),
             jax.ShapeDtypeStruct((users, events, STRETCH), BF16),
@@ -670,7 +700,7 @@
             pltpu.VMEM((items, width), BF16),
             pltpu.VMEM((width, full), BF16),
             pltpu.VMEM((width, inner), BF16),
-            pltpu.VMEM(w_out.shape, BF16),
+            pltpu.VMEM((CHUNK, w_out.shape[1]), BF16),
             pltpu.VMEM((1, inner), F32),
             pltpu.VMEM(conv_taps.shape, F32),
             pltpu.VMEM((users, stretches, 2 * heads, STRETCH), F32),
@@ -693,7 +723,7 @@
             pltpu.VMEM((ROWS, users, 1, pair), F32),
             pltpu.VMEM((users, ROWS, STRETCH, pair), BF16),
             pltpu.VMEM((ROWS, users, 1, pair), F32),
-            pltpu.VMEM((users, ROWS - 1, STRETCH, pair), F32),
+            pltpu.VMEM((ROWS - 1, ZS, users, part, pair), F32),
             pltpu.VMEM((ZS, users, part, pair), BF16),
             pltpu.VMEM((ZS, users, part, pair), BF16),
             pltpu.VMEM((ZS - 1, users, part, pair), F32),
@@ -705,7 +735,7 @@
             pltpu.VMEM((YS, users, 1, pair), F32),
             pltpu.VMEM((ZS, users, part, pair), BF16),
             pltpu.VMEM((ZS, users, part, pair), BF16),
-            pltpu.VMEM((users, ROWS, STRETCH, pair), BF16),
+            pltpu.VMEM((ROWS, ZS, users, part, pair), BF16),
             dma((16,)),
             pltpu.SemaphoreType.REGULAR((4,)),
             dma,
@@ -716,7 +746,7 @@
         + [dma((ZS,))] * 4
         + [dma((YS,))] * 4
         + [dma((ZS,))] * 2
-        + [dma((users, ROWS))] * 2,
+        + [dma((ROWS, ZS))] * 2,
         compiler_params=pltpu.CompilerParams(
             collective_id=0, has_side_effects=True, vmem_limit_bytes=36 << 20
         ),
@@ -746,7 +776,8 @@
         in_specs=[vmem] * 9,
         out_specs=hbm,
         scratch_shapes=[
-            pltpu.VMEM((events, CHUNK), BF16),
+            pltpu.VMEM((users, events, 3 * CHUNK), BF16),
+            pltpu.VMEM((users, events, STRETCH), F32),
             pltpu.VMEM((users, events, w_out.shape[1]), BF16),
             dma((users, w_out.shape[1] // CHUNK)),
         ],

time: 47.1 us -> 46.8 us (level)
    pallas_call x1, Pallas kernels: 44.2 us -> 41.9 us  [per_device(): pl.pallas_call(main_kernel, name='main', out_shape=(jax.ShapeDtypeStruct(...]
    pallas_call x1, Pallas kernels: 2.21 us -> 4.16 us  [per_device(): pl.pallas_call(final_kernel, name='final', out_shape=jax.ShapeDtypeStruct...]
where the time goes in v5:
time: 46.8 us; the launch traced here: 46.2 us
  Pallas kernels  46 us (98%)
    pallas_call x1, Pallas kernels, per_device(): pl.pallas_call(main_kernel, name='main', out_shape=(jax.ShapeDtypeStruct(...  41.9 us
    pallas_call x1, Pallas kernels, per_device(): pl.pallas_call(final_kernel, name='final', out_shape=jax.ShapeDtypeStruct...  4.16 us

profile of v5, /device:TPU:8, one launch (start us, length us, event | category | flops | bytes accessed | tf_op | source)
XLA Modules:
  0.0 46.2 jit_solution(7301745402328951011)
XLA Ops:
  0.0 0.0 copy-start
  0.0 0.0 copy-start.1
  0.0 41.9 %main.1 = (bf16[4,8,2,16,256]{4,3,2,1,0:T(8,128)(2,1)S(1)}, bf16[2,512,1024]{2,1,0:T(8,128)(2,1)S(1)}, bf16[2,512,1024]{2,1,0:T(8,128)(2,1)S(1)}, bf16[2,512,128...) custom-call(s32[2]{0:T(128)} %lengths_in.1, ...), custom_call_target="tpu_custom_call" | custom-call | tf_op jit(solution)/shard_map/main/pallas_call | solution.py:678
  41.9 0.0 copy-done
  41.9 0.0 copy-done.1
  41.9 4.2 %final.1 = bf16[2,1,512,1024]{3,2,1,0:T(8,128)(2,1)} custom-call(bf16[4,8,2,16,256]{4,3,2,1,0:T(8,128)(2,1)S(1)} %get-tuple-element.12.carry, bf16[2,512,1024]{2,1,0:T(8,128)(2,1)S(1)} %get-tuple-element.13.mix, bf16[2,512,1024]{2,1,0:T(8,128)(2,1)S(1)} %get-tuple-element.14.gate, bf16[2,512,128]{2,1,0:T(8,128)(2,1)S(1)} %get-tuple-element.15.outward, ...), custom_call_target="tpu_custom_call" | custom-call | tf_op jit(solution)/shard_map/final/pallas_call | solution.py:772
Async XLA Ops:
  0.0 41.9 %copy-start = (bf16[1024,1024]{1,0:T(8,128)(2,1)S(1)}, bf16[1024,1024]{1,0:T(8,128)(2,1)}, u32[]{:S(2)}) copy-start(bf16[1024,1024]{1,0:T(8,128)(2,1)} %w_out.1) | copy-start | bytes 6291460
  0.0 41.9 %copy-start.1 = (f32[1024]{0:T(1024)S(1)}, f32[1024]{0:T(1024)}, u32[]{:S(2)}) copy-start(f32[1024]{0:T(1024)} %param.22) | copy-start | bytes 12292

commit v6 on v5

--- a/solution.py
+++ b/solution.py
@@ -311,6 +311,13 @@
     ]
     row_logs[r] = logs[r]
 
+    for load in loads[10:13]:
+        load.wait()
+    for d in (1, 3, 0):
+        project(d, share(d))
+    pl.semaphore_wait(near.at[1], 2)
+    tell(2, sides)
+
     halo_copy.wait_recv()
     nobody = jnp.logical_and(r == 0, col == 0)
     for u in range(users):
@@ -371,15 +378,8 @@
     make_maps(0)
     gather(0, 2)
     make_maps(1)
-    state_step(0)
-    for load in loads[10:13]:
-        load.wait()
-    pl.semaphore_wait(near.at[1], 2)
-    tell(2, sides)
-    project(1, share(1))
-    state_step(1)
-    project(3, share(3))
-    state_step(2)
+    for i in range(3):
+        state_step(i)
 
     for copy in xl_copies:
         copy.wait_recv()
@@ -394,20 +394,8 @@
         send(z_log_out, z_logs.at[z], zl_send.at[d], zl_recv.at[d], to_z(d)) for d in range(1, ZS)
     ]
 
-    project(0, share(0))
     for i in range(3, len(order)):
         state_step(i)
-
-    for copy in zl_copies:
-        copy.wait_recv()
-    y_log = z_logs[0]
-    for i in range(1, ZS):
-        y_log = y_log + z_logs[i]
-    y_log_out[...] = y_log
-    y_logs[y] = y_log
-    yl_copies = [
-        send(y_log_out, y_logs.at[y], yl_send.at[d], yl_recv.at[d], to_y(d)) for d in range(1, YS)
-    ]
 
     loads[13].wait()
 
@@ -466,7 +454,18 @@
     ]
 
     gate_phase(shares // 2, shares)
-    local_phase(0, 0, 2)
+    local_phase(0, 0, 3)
+
+    for copy in zl_copies:
+        copy.wait_recv()
+    y_log = z_logs[0]
+    for i in range(1, ZS):
+        y_log = y_log + z_logs[i]
+    y_log_out[...] = y_log
+    y_logs[y] = y_log
+    yl_copies = [
+        send(y_log_out, y_logs.at[y], yl_send.at[d], yl_recv.at[d], to_y(d)) for d in range(1, YS)
+    ]
 
     for copy in z_copies:
         copy.wait_recv()
@@ -479,7 +478,8 @@
         send(y_out, y_states.at[y], y_send.at[d], y_recv.at[d], to_y(d)) for d in (2, 1, 3)
     ]
 
-    local_phase(0, 2, stretches)
+    local_phase(0, 3, stretches)
+    local_phase(1, 0, 2)
 
     for copy in yl_copies:
         copy.wait_recv()
@@ -528,8 +528,8 @@
             )
 
     forward(0)
-    local_phase(1, 0, 2)
-    for begin, ends in ((2, (1, 7)), (3, (2, 6)), (4, (3, 5, 4))):
+    local_phase(1, 2, 3)
+    for begin, ends in ((3, (1, 7)), (4, (2, 6)), (4, (3, 5, 4))):
         for d in ends:
             c_copies[d].wait_recv()
             forward(d)

time: 46.8 us -> 45.1 us (0.964)
  Pallas kernels: 46 us -> 44 us
    pallas_call x1, Pallas kernels: 41.9 us -> 39.8 us  [per_device(): pl.pallas_call(main_kernel, name='main', out_shape=(jax.ShapeDtypeStruct(...]
where the time goes in v6:
time: 45.1 us; the launch traced here: 44.2 us
  Pallas kernels  44 us (98%)
    pallas_call x1, Pallas kernels, per_device(): pl.pallas_call(main_kernel, name='main', out_shape=(jax.ShapeDtypeStruct(...  39.8 us
    pallas_call x1, Pallas kernels, per_device(): pl.pallas_call(final_kernel, name='final', out_shape=jax.ShapeDtypeStruct...  4.17 us

profile of v6, /device:TPU:8, one launch (start us, length us, event | category | flops | bytes accessed | tf_op | source)
XLA Modules:
  0.0 44.2 jit_solution(3087161631927588404)
XLA Ops:
  0.0 0.0 copy-start
  0.0 0.0 copy-start.1
  0.0 39.8 %main.1 = (bf16[4,8,2,16,256]{4,3,2,1,0:T(8,128)(2,1)S(1)}, bf16[2,512,1024]{2,1,0:T(8,128)(2,1)S(1)}, bf16[2,512,1024]{2,1,0:T(8,128)(2,1)S(1)}, bf16[2,512,128...) custom-call(s32[2]{0:T(128)} %lengths_in.1, ...), custom_call_target="tpu_custom_call" | custom-call | tf_op jit(solution)/shard_map/main/pallas_call | solution.py:678
  39.9 0.0 copy-done
  39.9 0.0 copy-done.1
  39.9 4.2 %final.1 = bf16[2,1,512,1024]{3,2,1,0:T(8,128)(2,1)} custom-call(bf16[4,8,2,16,256]{4,3,2,1,0:T(8,128)(2,1)S(1)} %get-tuple-element.12.carry, bf16[2,512,1024]{2,1,0:T(8,128)(2,1)S(1)} %get-tuple-element.13.mix, bf16[2,512,1024]{2,1,0:T(8,128)(2,1)S(1)} %get-tuple-element.14.gate, bf16[2,512,128]{2,1,0:T(8,128)(2,1)S(1)} %get-tuple-element.15.outward, ...), custom_call_target="tpu_custom_call" | custom-call | tf_op jit(solution)/shard_map/final/pallas_call | solution.py:772
Async XLA Ops:
  0.0 39.9 %copy-start = (bf16[1024,1024]{1,0:T(8,128)(2,1)S(1)}, bf16[1024,1024]{1,0:T(8,128)(2,1)}, u32[]{:S(2)}) copy-start(bf16[1024,1024]{1,0:T(8,128)(2,1)} %w_out.1) | copy-start | bytes 6291460
  0.0 39.9 %copy-start.1 = (f32[1024]{0:T(1024)S(1)}, f32[1024]{0:T(1024)}, u32[]{:S(2)}) copy-start(f32[1024]{0:T(1024)} %param.22) | copy-start | bytes 12292

commit v7 on v6

--- a/solution.py
+++ b/solution.py
@@ -7,6 +7,7 @@
 
 STRETCH = 128
 CHUNK = 256
+WIDE = 512
 HALO = 16
 ROWS, YS, ZS = 4, 4, 8
 MESH = pl.DeviceIdType.MESH
@@ -117,7 +118,6 @@
     inner = w_gate.shape[1]
     heads = w_dt.shape[0]
     stretches = events // STRETCH
-    shares = inner // CHUNK
     part = z_states.shape[2]
     r = lax.axis_index("row")
     col = lax.axis_index("col")
@@ -325,16 +325,16 @@
 
     joined = (joined_even, joined_odd)
 
-    def gather(u, slot):
+    def gather(u, slot, turn):
         rows = dot(hot[u], projected[slot])
         for half in range(2):
-            joined[u][half] = rows[:, half * STRETCH : (half + 1) * STRETCH]
-
-    def convolve(u, half, weights, columns):
+            joined[turn][half] = rows[:, half * STRETCH : (half + 1) * STRETCH]
+
+    def convolve(turn, half, weights, columns):
         total = None
         for k in range(weights.shape[0]):
             begin = HALO - weights.shape[0] + 1 + k
-            term = joined[u][half, begin : begin + events, :] * weights[k : k + 1, columns]
+            term = joined[turn][half, begin : begin + events, :] * weights[k : k + 1, columns]
             total = term if total is None else total + term
         return total
 
@@ -347,15 +347,16 @@
             in_rows[u, :, rows] = jnp.transpose(into[rows].astype(F32))
 
     x_copies = {}
-    order = [(d, u) for d in shares_order for u in range(users)]
+    order = [(d, u) for u in range(users) for d in shares_order[:3]]
+    order += [(0, u) for u in range(users)]
 
     def state_step(i, prefetch=True):
         d, u = order[i]
         if prefetch and i + 1 < len(order):
-            gather(order[i + 1][1], order[i + 1][0])
+            gather(order[i + 1][1], order[i + 1][0], (i + 1) % 2)
         for half in range(2):
             columns = share(d, half * STRETCH, STRETCH)
-            values = silu_of_half(convolve(u, half, half_taps, columns)).astype(BF16)
+            values = silu_of_half(convolve(i % 2, half, half_taps, columns)).astype(BF16)
             signal[u, :, columns] = values
             scaled = (in_rows[u] * tails[u, 2 * row_peer(d) + half]).astype(BF16)
             state = dot(scaled, values).astype(BF16)
@@ -373,10 +374,10 @@
                 to_row(d),
             )
 
-    gather(0, ROWS)
-    gather(1, ROWS)
+    gather(0, ROWS, 0)
+    gather(1, ROWS, 1)
     make_maps(0)
-    gather(0, 2)
+    gather(0, 2, 0)
     make_maps(1)
     for i in range(3):
         state_step(i)
@@ -402,7 +403,7 @@
     def gate_phase(begin, end):
         @pl.loop(begin, end)
         def _(j):
-            columns = pl.ds(pl.multiple_of(j * CHUNK, CHUNK), CHUNK)
+            columns = pl.ds(pl.multiple_of(j * WIDE, WIDE), WIDE)
             opened = dot(table[...], w_gate[:, columns]).astype(BF16)
             opened = silu_of_half(0.5 * opened.astype(F32)).astype(BF16)
             for u in range(users):
@@ -434,7 +435,7 @@
                 scaled = (in_t * tail_t[h : h + 1, :]).astype(BF16)
                 running[:, cols] = stay[h : h + 1, :] * entering + dot(scaled, values)
 
-    gate_phase(0, shares // 2)
+    gate_phase(0, 1)
 
     for u in range(users):
         for d in range(1, ROWS):
@@ -453,7 +454,7 @@
         for d in (4, 3, 5, 2, 6, 1, 7)
     ]
 
-    gate_phase(shares // 2, shares)
+    gate_phase(1, inner // WIDE)
     local_phase(0, 0, 3)
 
     for copy in zl_copies:

time: 45.1 us -> 45.2 us (level)
  no operation moved by 1% of the time
where the time goes in v7:
time: 45.2 us; the launch traced here: 44.5 us
  Pallas kernels  44.3 us (98%)
    pallas_call x1, Pallas kernels, per_device(): pl.pallas_call(main_kernel, name='main', out_shape=(jax.ShapeDtypeStruct(...  40.1 us
    pallas_call x1, Pallas kernels, per_device(): pl.pallas_call(final_kernel, name='final', out_shape=jax.ShapeDtypeStruct...  4.17 us

profile of v7, /device:TPU:8, one launch (start us, length us, event | category | flops | bytes accessed | tf_op | source)
XLA Modules:
  0.0 44.5 jit_solution(18060618207704646396)
XLA Ops:
  0.0 0.0 copy-start
  0.0 0.0 copy-start.1
  0.0 40.1 %main.1 = (bf16[4,8,2,16,256]{4,3,2,1,0:T(8,128)(2,1)S(1)}, bf16[2,512,1024]{2,1,0:T(8,128)(2,1)S(1)}, bf16[2,512,1024]{2,1,0:T(8,128)(2,1)S(1)}, bf16[2,512,128...) custom-call(s32[2]{0:T(128)} %lengths_in.1, ...), custom_call_target="tpu_custom_call" | custom-call | tf_op jit(solution)/shard_map/main/pallas_call | solution.py:679
  40.1 0.0 copy-done
  40.2 0.0 copy-done.1
  40.2 4.2 %final.1 = bf16[2,1,512,1024]{3,2,1,0:T(8,128)(2,1)} custom-call(bf16[4,8,2,16,256]{4,3,2,1,0:T(8,128)(2,1)S(1)} %get-tuple-element.12.carry, bf16[2,512,1024]{2,1,0:T(8,128)(2,1)S(1)} %get-tuple-element.13.mix, bf16[2,512,1024]{2,1,0:T(8,128)(2,1)S(1)} %get-tuple-element.14.gate, bf16[2,512,128]{2,1,0:T(8,128)(2,1)S(1)} %get-tuple-element.15.outward, ...), custom_call_target="tpu_custom_call" | custom-call | tf_op jit(solution)/shard_map/final/pallas_call | solution.py:773
Async XLA Ops:
  0.0 40.1 %copy-start = (bf16[1024,1024]{1,0:T(8,128)(2,1)S(1)}, bf16[1024,1024]{1,0:T(8,128)(2,1)}, u32[]{:S(2)}) copy-start(bf16[1024,1024]{1,0:T(8,128)(2,1)} %w_out.1) | copy-start | bytes 6291460
  0.0 40.2 %copy-start.1 = (f32[1024]{0:T(1024)S(1)}, f32[1024]{0:T(1024)}, u32[]{:S(2)}) copy-start(f32[1024]{0:T(1024)} %param.22) | copy-start | bytes 12292
